TPU v7x, 256 devices: a whole 4x4x8 slice. The times are simulated.
256 devices in a mesh: dp: 8 (over x, core), rows: 32 (over y, z).
Axes of the slice: x: 4, y: 4, z: 8, core: 2. Of those that a mesh axis runs over, the one named last changes fastest.
Arguments:
- grads: bfloat16 [2, 4096, 14336], P(None, 'rows', 'dp'), may hold values from -64 to 64
- basis: bfloat16 [2, 4096, 512], P(None, 'rows'), may hold values from -0.09375 to 0.09375
- moment1: float32 [2, 512, 14336], P(None, 'rows', 'dp'), may hold values from -0.3 to 0.3
- moment2: float32 [2, 512, 14336], P(None, 'rows', 'dp'), may hold values from 0.001 to 0.03
- weights: bfloat16 [2, 4096, 14336], P(None, 'rows', 'dp'), may hold values from -0.09375 to 0.09375
Outputs:
- new_weights: bfloat16 [2, 4096, 14336], P(None, 'rows')
- new_moment1: float32 [2, 512, 14336], P(None, 'rows', 'dp')
- new_moment2: float32 [2, 512, 14336], P(None, 'rows', 'dp')
All inputs are finite; a program needn't handle non-finite values.
Results may differ from a plain program's by a relative error of at most 0.00115.
The roundings to bfloat16 on the way count: a program that leaves them out, or rounds other values in their place, can miss the bound.
Values may be sent and summed in bfloat16 or wider, within the bound.
No kernel may reach another device: no remote copies, remote signals or barrier semaphores. Data moves between devices by JAX's collectives and lax.ppermute only.
A program may use at most 64 MiB of HBM per device.

v0:
```python
import functools
import math

import jax
import jax.numpy as jnp
from jax import lax
from jax.experimental import pallas as pl
from jax.experimental.pallas import tpu as pltpu
from jax.sharding import Mesh
from jax.sharding import PartitionSpec as P


D = 4096
FF = 14336
MATS = 2
STEP = 10
F32 = jnp.float32
BF16 = jnp.bfloat16
VMEM = pl.BlockSpec(memory_space=pltpu.VMEM)
SMEM = pl.BlockSpec(memory_space=pltpu.SMEM)
ANY = pl.BlockSpec(memory_space=pl.ANY)
PARAMS = pltpu.CompilerParams(vmem_limit_bytes=8 * 2**20)


def shift(v, axis, k):
    n = lax.axis_size(axis)
    return lax.ppermute(v, axis, [(i, (i + k) % n) for i in range(n)])


def exchange(v, axis):
    return lax.all_to_all(v, axis, split_axis=0, concat_axis=0, tiled=True)


def cost(flops, size):
    return pl.CostEstimate(flops=int(flops), bytes_accessed=int(size), transcendentals=0)


def before(first, second):
    return lax.optimization_barrier((first, second))[1]


def pack_kernel(v_ref, out_ref):
    nz, _, cols, _ = out_ref.shape
    for m in range(MATS):
        turned = jnp.transpose(v_ref[m])
        for z in range(nz):
            out_ref[z, m] = turned[z * cols : (z + 1) * cols]


def pack(v, nz):
    mats, rows, cols = v.shape
    return pl.pallas_call(
        pack_kernel,
        out_shape=jax.ShapeDtypeStruct((nz, mats, cols // nz, rows), BF16),
        in_specs=[VMEM],
        out_specs=VMEM,
        compiler_params=PARAMS,
        cost_estimate=cost(2e9, 2 * 2**20),
        name="pack",
    )(v)


def pieces_kernel(at_ref, v_ref, basis_ref, out_ref):
    nz, size, width = out_ref.shape
    part = basis_ref.shape[1] // 8
    start = pl.multiple_of((at_ref[0] * 2 + at_ref[1]) * part, part)
    total = None
    for m in range(MATS):
        wide = v_ref[m].astype(F32)
        squares = jnp.sum(wide * wide, axis=0, keepdims=True)
        total = squares if total is None else total + squares
        piece = basis_ref[m, pl.ds(start, part)]
        count = piece.shape[1] // width
        for k in range(count):
            low = (m * count + k) * part
            for z in range(nz):
                out_ref[z, low : low + part] = piece[:, k * width : (k + 1) * width]
    total = jnp.sum(total, axis=1, keepdims=True)
    high = total.astype(BF16).astype(F32)
    middle = (total - high).astype(BF16).astype(F32)
    low = total - high - middle
    row = lax.broadcasted_iota(jnp.int32, (part, width), 0)
    tile = jnp.where(row == 0, high, jnp.where(row == 1, middle, jnp.where(row == 2, low, 0.0)))
    for z in range(nz):
        out_ref[z, size - part :] = tile.astype(BF16)


def pieces(at, v, basis, nz):
    mats, rows, rank = basis.shape
    part, width = rows // 8, 128
    return pl.pallas_call(
        pieces_kernel,
        out_shape=jax.ShapeDtypeStruct((nz, mats * part * rank // width + part, width), BF16),
        in_specs=[SMEM, VMEM, VMEM],
        out_specs=VMEM,
        compiler_params=PARAMS,
        cost_estimate=cost(2e9, 2**20),
        name="pieces",
    )(at, v, basis)


def pack_state_kernel(at_ref, one_ref, two_ref, *refs):
    outs, held_ref = refs[:-1], refs[-1]
    nz, _, cols = held_ref.shape
    ranks = one_ref.shape[1]
    for k, ref in enumerate((one_ref, two_ref)):
        for m in range(MATS):
            low = (k * MATS + m) * ranks
            for z in range(nz):
                held_ref[z, low : low + ranks] = ref[m, :, z * cols : (z + 1) * cols]
    for d in range(nz):
        outs[d][...] = held_ref[lax.rem(at_ref[3] + d, nz)]


def pack_state(at, one, two, nz):
    mats, ranks, cols = one.shape
    size = (2 * mats * ranks, cols // nz)
    return pl.pallas_call(
        pack_state_kernel,
        out_shape=[jax.ShapeDtypeStruct(size, F32)] * nz,
        in_specs=[SMEM, VMEM, VMEM],
        out_specs=[VMEM] * nz,
        scratch_shapes=[pltpu.VMEM((nz, *size), F32)],
        compiler_params=PARAMS,
        cost_estimate=cost(2e9, 2**20),
        name="pack_state",
    )(at, one, two)


def unpack_state_kernel(in_ref, one_ref, two_ref):
    nz, _, _ = in_ref.shape
    ranks = one_ref.shape[1]
    for k, ref in enumerate((one_ref, two_ref)):
        for m in range(MATS):
            low = (k * MATS + m) * ranks
            ref[m] = jnp.concatenate([in_ref[z, low : low + ranks] for z in range(nz)], axis=1)


def unpack_state(held):
    nz, kinds, cols = held.shape
    shape = jax.ShapeDtypeStruct((MATS, kinds // (2 * MATS), nz * cols), F32)
    return pl.pallas_call(
        unpack_state_kernel,
        out_shape=[shape, shape],
        in_specs=[VMEM],
        out_specs=[VMEM] * 2,
        compiler_params=PARAMS,
        cost_estimate=cost(2e9, 2**20),
        name="unpack_state",
    )(held)


def project_kernel(at_ref, g_ref, own_ref, peer_ref, basis_ref, *refs):
    outs, total_ref = refs[:-1], refs[-1]
    x, core, y = (at_ref[i] for i in range(3))
    nx, nz, size, width = own_ref.shape
    rank = basis_ref.shape[3]
    part = basis_ref.shape[2] // (2 * nx)
    count = rank // width
    cols = g_ref.shape[2]
    ny = len(outs)

    def gather(z, _):
        for m in range(MATS):
            for xa in range(nx):
                d = lax.rem(x - xa + nx, nx)
                for k in range(count):
                    low = (m * count + k) * part
                    ours, theirs = own_ref[d, z, low : low + part], peer_ref[d, z, low : low + part]
                    at = 2 * xa * part
                    lanes = slice(k * width, (k + 1) * width)
                    basis_ref[m, z, at : at + part, lanes] = jnp.where(core == 0, ours, theirs)
                    basis_ref[m, z, at + part : at + 2 * part, lanes] = jnp.where(
                        core == 0, theirs, ours
                    )
        return 0

    lax.fori_loop(0, nz, gather, 0)

    def multiply(m, _):
        left = jnp.concatenate([g_ref[z, m] for z in range(nz)], axis=1)
        right = basis_ref[m].reshape(left.shape[1], -1)
        total_ref[m] = jnp.dot(left, right, preferred_element_type=F32)
        return 0

    lax.fori_loop(0, MATS, multiply, 0)
    squares = jnp.zeros((part, width), F32)
    for ref in (own_ref, peer_ref):
        for d in range(nx):
            for z in range(nz):
                squares = squares + ref[d, z, size - part :].astype(F32)
    squares = jnp.sum(squares, axis=0, keepdims=True)
    for d in range(ny):
        start = pl.multiple_of(lax.rem(y + d, ny) * width, width)
        outs[d][:, :cols] = total_ref[:, :, pl.ds(start, width)]
        for m in range(MATS):
            outs[d][m, cols:] = jnp.broadcast_to(squares, (8, width))


def project(at, g, own, peer, rank, parts):
    nz, mats, cols, rows = g.shape
    basis, *out = pl.pallas_call(
        project_kernel,
        out_shape=[jax.ShapeDtypeStruct((mats, nz, rows, rank), BF16)]
        + [jax.ShapeDtypeStruct((mats, cols + 8, rank // parts), F32)] * parts,
        in_specs=[SMEM] + [VMEM] * 3,
        out_specs=[VMEM] * (1 + parts),
        scratch_shapes=[pltpu.VMEM((mats, cols, rank), F32)],
        compiler_params=PARAMS,
        cost_estimate=cost(2 * mats * nz * cols * rows * rank, 4 * 2**20),
        name="project",
    )(at, g, own, peer)
    return basis, out


def moments_kernel(at_ref, sum_ref, *refs):
    held, new_ref, update_ref, held_ref = refs[:-3], refs[-3], refs[-2], refs[-1]
    nz, kinds, cols = held_ref.shape
    ranks = kinds // (2 * MATS)
    for d in range(nz):
        held_ref[lax.rem(at_ref[3] - d + nz, nz)] = held[d][...]
    limit = 1.0 * math.sqrt(MATS * D * FF)
    scale = limit / jnp.maximum(jnp.sqrt(sum_ref[0, cols : cols + 1, 0:1]), limit)
    first_bias_correction = 1.0 - 0.9**STEP
    second_fix = 1.0 - 0.999**STEP
    spare = 256 - cols
    for m in range(MATS):
        one, two = (slice(k * ranks, (k + 1) * ranks) for k in (m, MATS + m))
        summed = sum_ref[m, :cols]
        padded = jnp.concatenate([summed, jnp.zeros((spare, summed.shape[1]), F32)], axis=0)
        scaled = scale * jnp.transpose(padded)[:, :cols]
        first = 0.9 * held_ref[:, one].reshape(nz * ranks, cols) + 0.1 * scaled
        second = 0.999 * held_ref[:, two].reshape(nz * ranks, cols) + 0.001 * scaled * scaled
        new_ref[:, one] = first.reshape(nz, ranks, cols)
        new_ref[:, two] = second.reshape(nz, ranks, cols)
        update = first / first_bias_correction / (jnp.sqrt(second / second_fix) + 1e-08)
        wide = jnp.concatenate([update, jnp.zeros((update.shape[0], spare), F32)], axis=1)
        update_ref[m] = jnp.transpose(wide)[:cols].astype(BF16)


def moments(at, summed, held):
    nz = len(held)
    kinds, cols = held[0].shape
    ranks = kinds // (2 * MATS)
    return pl.pallas_call(
        moments_kernel,
        out_shape=[
            jax.ShapeDtypeStruct((nz, kinds, cols), F32),
            jax.ShapeDtypeStruct((MATS, cols, nz * ranks), BF16),
        ],
        in_specs=[SMEM] + [VMEM] * (1 + nz),
        out_specs=[VMEM] * 2,
        scratch_shapes=[pltpu.VMEM((nz, kinds, cols), F32)],
        compiler_params=PARAMS,
        cost_estimate=cost(2e9, 2 * 2**20),
        name="moments",
    )(at, summed, *held)


def back_kernel(m, at_ref, basis_ref, w_ref, u0, u1, u2, u3, *refs):
    outs, whole_ref = refs[:-1], refs[-1]
    y, here = at_ref[2], at_ref[3]
    nz = basis_ref.shape[1]
    width = u0.shape[2]
    blocks = (u0, u1, u2, u3)
    n = len(blocks)
    for d in range(n):
        start = pl.multiple_of(lax.rem(y - d + n, n) * width, width)
        whole_ref[:, pl.ds(start, width)] = blocks[d][m]

    def rows(z):
        product = lax.dot_general(
            whole_ref[...], basis_ref[m, z], (((1,), (1,)), ((), ())), preferred_element_type=F32
        )
        return (w_ref[z, m].astype(F32) - 0.5 * product).astype(BF16)

    if len(outs) == 1:

        def store(z, _):
            outs[0][z] = rows(z)
            return 0

        lax.fori_loop(0, nz, store, 0)
    else:
        for d in range(nz):
            outs[d][...] = rows(lax.rem(here + d, nz))


def back(m, at, basis, w, blocks, apart):
    nz, _, cols, rows = w.shape
    rank = basis.shape[3]
    shapes = [(cols, rows)] * nz if apart else [(nz, cols, rows)]
    return pl.pallas_call(
        functools.partial(back_kernel, m),
        out_shape=[jax.ShapeDtypeStruct(shape, BF16) for shape in shapes],
        in_specs=[SMEM] + [VMEM] * 6,
        out_specs=[VMEM] * len(shapes),
        scratch_shapes=[pltpu.VMEM((cols, rank), BF16)],
        compiler_params=PARAMS,
        cost_estimate=cost(2 * nz * rows * cols * rank, 3 * 2**20),
        name="back",
    )(at, basis, w, *blocks)


def turn_kernel(at_ref, *refs):
    blocks, out_ref, held_ref = refs[:-2], refs[-2], refs[-1]
    nz, cols, rows = held_ref.shape
    for d in range(nz):
        held_ref[lax.rem(at_ref[3] - d + nz, nz)] = blocks[d][...]
    out_ref[...] = jnp.transpose(held_ref[...].reshape(nz * cols, rows))


def turn(at, blocks):
    nz = len(blocks)
    cols, rows = blocks[0].shape
    return pl.pallas_call(
        turn_kernel,
        out_shape=jax.ShapeDtypeStruct((rows, nz * cols), BF16),
        in_specs=[SMEM] + [VMEM] * nz,
        out_specs=VMEM,
        scratch_shapes=[pltpu.VMEM((nz, cols, rows), BF16)],
        compiler_params=PARAMS,
        cost_estimate=cost(2e9, 2**20),
        name="turn",
    )(at, *blocks)


def place_kernel(m, spots, at_ref, *refs):
    n = len(spots)
    blocks, out_ref, sems = refs[:n], refs[-2], refs[-1]
    x, core = at_ref[0], at_ref[1]
    copies = []
    for i, (dx, across, row) in enumerate(spots):
        rows, width = blocks[i].shape
        owner = lax.rem(x + dx, 4) * 2 + (1 - core if across else core)
        start = pl.multiple_of(owner * width, 128)
        copies.append(
            pltpu.make_async_copy(
                blocks[i], out_ref.at[m, pl.ds(row, rows), pl.ds(start, width)], sems.at[i]
            )
        )
    for copy in copies:
        copy.start()
    for copy in copies:
        copy.wait()


def place(whole, shape, m, at, items):
    spots = [item[1:] for item in items]
    blocks = [item[0] for item in items]
    n = len(blocks)
    given = () if whole is None else (whole,)
    size = sum(2 * 2 * b.size for b in blocks)
    return pl.pallas_call(
        functools.partial(place_kernel, m, spots),
        out_shape=jax.ShapeDtypeStruct(shape, BF16),
        in_specs=[SMEM] + [VMEM] * n + [ANY] * len(given),
        out_specs=ANY,
        scratch_shapes=[pltpu.SemaphoreType.DMA((n,))],
        input_output_aliases={} if whole is None else {n + 1: 0},
        compiler_params=PARAMS,
        cost_estimate=cost(2e9, size),
        name="place",
    )(at, *blocks, *given)


def step(grads, basis, moment1, moment2, weights):
    x, core = lax.axis_index("x"), lax.axis_index("core")
    y, z = lax.axis_index("y"), lax.axis_index("z")
    nx, nc, ny, nz = (lax.axis_size(a) for a in ("x", "core", "y", "z"))
    mats, rows, cols = grads.shape
    rank = basis.shape[2]
    at = jnp.stack([x, core, y, z])

    held = exchange(pieces(at, grads, basis, nz), "z")
    sent = pack(grads, nz)
    mine = exchange(sent, "z")
    w = pack(weights, nz)
    state = pack_state(at, moment1, moment2, nz)
    own = jnp.stack([held] + [shift(held, "x", k) for k in range(1, nx)])
    peer = shift(own, "core", 1)
    state = [state[0]] + [shift(state[k], "z", k) for k in range(1, nz)]
    w = exchange(before(mine, w), "z")

    gathered, parts = project(at, mine, own, peer, rank, ny)
    parts = [parts[0]] + [shift(parts[k], "y", k) for k in range(1, ny)]
    summed = (parts[0] + parts[1]) + (parts[2] + parts[3])
    news, update = moments(at, summed, state)
    updates = [update] + [shift(update, "y", k) for k in range(1, ny)]
    whole_block = back(0, at, gathered, w, updates, False)[0]
    whole_block = exchange(whole_block, "z")
    blocks = back(1, at, gathered, w, updates, True)
    blocks = [blocks[0]] + [shift(blocks[k], "z", k) for k in range(1, nz)]
    fresh = [jnp.swapaxes(whole_block.reshape(cols, rows), 0, 1), turn(at, blocks)]
    news = exchange(before(whole_block, news), "z")
    news = unpack_state(news)

    half = rows // 2
    shape = (mats, rows, cols * nx * nc)

    def put(whole, m, items):
        there = [(shift(b, "core", 1), dx, True, row) for b, dx, row in items]
        here = [(b, dx, False, row) for b, dx, row in items]
        return place(whole, shape, m, at, here + there)

    near = []
    for f in fresh:
        near.append((shift(f, "x", 1), shift(f, "x", -1)))
    whole = put(None, 0, [(fresh[0], 0, 0)])
    whole = put(whole, 0, [(near[0][0], 3, 0), (near[0][1], 1, 0)])
    for m in range(mats):
        left, right = near[m]
        if m:
            whole, left, right = lax.optimization_barrier((whole, left, right))
            whole = put(whole, m, [(fresh[m], 0, 0)])
            whole = put(whole, m, [(left, 3, 0), (right, 1, 0)])
        top, low = shift(left[:half], "x", 1), shift(right[half:], "x", -1)
        if m:
            whole, top, low = lax.optimization_barrier((whole, top, low))
        whole = put(whole, m, [(top, 2, 0), (low, 2, half)])
    return (whole, news[0], news[1])


def solution(mesh):
    finer = Mesh(mesh.devices.reshape(4, 2, 4, 8), ("x", "core", "y", "z"))
    dp, rows = ("x", "core"), ("y", "z")
    in_specs = (
        P(None, rows, dp),
        P(None, rows, None),
        P(None, rows, dp),
        P(None, rows, dp),
        P(None, rows, dp),
    )
    out_specs = (P(None, rows, None), P(None, rows, dp), P(None, rows, dp))
    return jax.shard_map(step, mesh=finer, in_specs=in_specs, out_specs=out_specs, check_vma=False)
```

profile of v0, /device:TPU:1, one launch (start us, length us, event | category | flops | bytes accessed | tf_op | source)
XLA Modules:
  0.0 201.7 jit_solution(12475969192650466151)
XLA Ops:
  2.8 1.4 pieces.1
  4.3 9.0 %all-to-all-start.1 = ((bf16[8,144,128]{2,1,0:T(8,128)(2,1)}), bf16[8,144,128]{2,1,0:T(8,128)(2,1)S(1)}, u32[]{:S(2)}, u32[]{:S(2)}) async-start(bf16[8,144,128]{2,1,0:T(8,128)(2,1)} %pieces.1), calls=%async_computation.1 | async-start | bytes 589824 | tf_op jit(solution)/shard_map/all_to_all | solution.py:31
  14.5 10.0 %all-to-all-done.1 = bf16[8,144,128]{2,1,0:T(8,128)(2,1)S(1)} async-done(((bf16[8,144,128]{2,1,0:T(8,128)(2,1)}), bf16[8,144,128]{2,1,0:T(8,128)(2,1)S(1)}, u32[]{:S(2)}, u32[]{:S(2)}) %all-to-all-start.1) | async-done | bytes 294944 | tf_op jit(solution)/shard_map/all_to_all | solution.py:31
  24.5 3.6 %all-to-all-start = ((bf16[8,2,224,128]{3,2,1,0:T(8,128)(2,1)}), bf16[8,2,224,128]{3,2,1,0:T(8,128)(2,1)S(1)}, u32[]{:S(2)}, u32[]{:S(2)}) async-start(bf16[8,2,224,128]{3,2,1,0:T(8,128)(2,1)} %pack.2), calls=%async_computation | async-start | bytes 1835008 | tf_op jit(solution)/shard_map/all_to_all | solution.py:31
  29.4 2.5 %collective-permute-start.1 = (bf16[8,144,128]{2,1,0:T(8,128)(2,1)S(1)}, bf16[8,144,128]{2,1,0:T(8,128)(2,1)S(1)}, u32[]{:S(2)}, u32[]{:S(2)}) collective-permute-start(bf16[8,144,128]{2,1,0:T(8,128)(2,1)S(1)} %all-to-all-done.1), channel_id=1, source_target_pairs={{0,128},{64,192},{128,0},{192,64},{1,129},{65,193},{129,1},{193,65... | collective-permute-start | bytes 884744 | tf_op jit(solution)/shard_map/ppermute | solution.py:27
  33.0 2.7 %collective-permute-done = bf16[8,144,128]{2,1,0:T(8,128)(2,1)S(1)} collective-permute-done((bf16[8,144,128]{2,1,0:T(8,128)(2,1)S(1)}, bf16[8,144,128]{2,1,0:T(8,128)(2,1)S(1)}, u32[]{:S(2)}, u32[]{:S(2)}) %collective-permute-start) | collective-permute-done | bytes 294944 | tf_op jit(solution)/shard_map/ppermute | solution.py:27
  35.7 7.3 %collective-permute-done.1 = bf16[8,144,128]{2,1,0:T(8,128)(2,1)S(1)} collective-permute-done((bf16[8,144,128]{2,1,0:T(8,128)(2,1)S(1)}, bf16[8,144,128]{2,1,0:T(8,128)(2,1)S(1)}, u32[]{:S(2)}, u32[]{:S(2)}) %collective-permute-start.1) | collective-permute-done | bytes 294944 | tf_op jit(solution)/shard_map/ppermute | solution.py:27
  43.5 2.8 %collective-permute-start.3 = (bf16[4,8,144,128]{3,2,1,0:T(8,128)(2,1)S(1)}, bf16[4,8,144,128]{3,2,1,0:T(8,128)(2,1)}, u32[]{:S(2)}, u32[]{:S(2)}) collective-permute-start(bf16[4,8,144,128]{3,2,1,0:T(8,128)(2,1)S(1)} %pad_maximum_fusion.own_ref), channel_id=1, source_target_pairs={{0,32},{32,0},{1,33},{33,1},{2,34},{34,2},{3,35},{35,3},{4,36},{36... | collective-permute-start | bytes 3538952 | tf_op jit(solution)/shard_map/ppermute | solution.py:27
  47.6 5.2 %all-to-all-done.g_ref = bf16[8,2,224,128]{3,2,1,0:T(8,128)(2,1)S(1)} async-done(((bf16[8,2,224,128]{3,2,1,0:T(8,128)(2,1)}), bf16[8,2,224,128]{3,2,1,0:T(8,128)(2,1)S(1)}, u32[]{:S(2)}, u32[]{:S(2)}) %all-to-all-start) | async-done | bytes 917536 | tf_op jit(solution)/shard_map/all_to_all | solution.py:31
  52.8 3.6 %all-to-all-start.2 = ((bf16[8,2,224,128]{3,2,1,0:T(8,128)(2,1)}), bf16[8,2,224,128]{3,2,1,0:T(8,128)(2,1)S(1)}, u32[]{:S(2)}, u32[]{:S(2)}) async-start(bf16[8,2,224,128]{3,2,1,0:T(8,128)(2,1)} %copy-done.4), calls=%async_computation.2 | async-start | bytes 1835008 | tf_op jit(solution)/shard_map/all_to_all | solution.py:31
  58.8 2.8 %project.1 = (bf16[2,8,128,512]{3,2,1,0:T(8,128)(2,1)S(1)}, f32[2,232,128]{2,1,0:T(8,128)S(1)}, f32[2,232,128]{2,1,0:T(8,128)S(1)}, f32[2,232,128]{2,1,0:T(8,128)S(1)}, f32[2,232,128]{2,1,0:T(8,128)S(1)}) custom-call(s32[4]{0:T(128)S(1)} %pad_add_fusion.at_ref, bf16[8,2,224,128]{3,2,1,0:T(8,128)(2,1)S(1)} %copy-done.3, ...), custom_call_target="tpu_custom_call" | custom-call | flops 469762048 | bytes 4194304 | tf_op jit(solution)/shard_map/project/pallas_call | solution.py:202
  61.6 1.4 collective-permute-start.4
  62.9 2.6 %collective-permute-start.5 = (f32[2,232,128]{2,1,0:T(8,128)S(1)}, f32[2,232,128]{2,1,0:T(8,128)S(1)}, u32[]{:S(2)}, u32[]{:S(2)}) collective-permute-start(f32[2,232,128]{2,1,0:T(8,128)S(1)} %get-tuple-element.40), channel_id=1, source_target_pairs={{0,16},{8,24},{16,0},{24,8},{1,17},{9,25},{17,1},{25,9},{2,18},{10... | collective-permute-start | bytes 712712 | tf_op jit(solution)/shard_map/ppermute | solution.py:27
  67.4 5.4 %collective-permute-start.10 = (f32[64,224]{1,0:T(8,128)S(1)}, f32[64,224]{1,0:T(8,128)S(1)}, u32[]{:S(2)}, u32[]{:S(2)}) collective-permute-start(f32[64,224]{1,0:T(8,128)S(1)} %get-tuple-element.46), channel_id=1, source_target_pairs={{0,4},{1,5},{2,6},{3,7},{4,0},{5,1},{6,2},{7,3},{8,12},{9,13},{10,... | collective-permute-start | bytes 172040 | tf_op jit(solution)/shard_map/ppermute | solution.py:27
  73.0 11.2 %collective-permute-done.10.refs_4_ = f32[64,224]{1,0:T(8,128)S(1)} collective-permute-done((f32[64,224]{1,0:T(8,128)S(1)}, f32[64,224]{1,0:T(8,128)S(1)}, u32[]{:S(2)}, u32[]{:S(2)}) %collective-permute-start.10) | collective-permute-done | bytes 57376 | tf_op jit(solution)/shard_map/ppermute | solution.py:27
  84.2 2.5 %collective-permute-start.13 = (f32[64,224]{1,0:T(8,128)S(1)}, f32[64,224]{1,0:T(8,128)S(1)}, u32[]{:S(2)}, u32[]{:S(2)}) collective-permute-start(f32[64,224]{1,0:T(8,128)S(1)} %get-tuple-element.49), channel_id=1, source_target_pairs={{0,7},{1,0},{2,1},{3,2},{4,3},{5,4},{6,5},{7,6},{8,15},{9,8},{10,9... | collective-permute-start | bytes 172040 | tf_op jit(solution)/shard_map/ppermute | solution.py:27
  86.8 2.8 %collective-permute-start.7 = (f32[64,224]{1,0:T(8,128)S(1)}, f32[64,224]{1,0:T(8,128)S(1)}, u32[]{:S(2)}, u32[]{:S(2)}) collective-permute-start(f32[64,224]{1,0:T(8,128)S(1)} %get-tuple-element.43), channel_id=1, source_target_pairs={{0,1},{1,2},{2,3},{3,4},{4,5},{5,6},{6,7},{7,0},{8,9},{9,10},{10,1... | collective-permute-start | bytes 172040 | tf_op jit(solution)/shard_map/ppermute | solution.py:27
  91.5 3.8 %collective-permute-done.8.refs_2_ = f32[64,224]{1,0:T(8,128)S(1)} collective-permute-done((f32[64,224]{1,0:T(8,128)S(1)}, f32[64,224]{1,0:T(8,128)S(1)}, u32[]{:S(2)}, u32[]{:S(2)}) %collective-permute-start.8) | collective-permute-done | bytes 57376 | tf_op jit(solution)/shard_map/ppermute | solution.py:27
  95.3 3.9 %collective-permute-done.9.refs_3_ = f32[64,224]{1,0:T(8,128)S(1)} collective-permute-done((f32[64,224]{1,0:T(8,128)S(1)}, f32[64,224]{1,0:T(8,128)S(1)}, u32[]{:S(2)}, u32[]{:S(2)}) %collective-permute-start.9) | collective-permute-done | bytes 57376 | tf_op jit(solution)/shard_map/ppermute | solution.py:27
  99.2 1.6 moments.1
  100.8 2.7 %collective-permute-start.16 = (bf16[2,224,128]{2,1,0:T(8,128)(2,1)S(1)}, bf16[2,224,128]{2,1,0:T(8,128)(2,1)S(1)}, u32[]{:S(2)}, u32[]{:S(2)}) collective-permute-start(bf16[2,224,128]{2,1,0:T(8,128)(2,1)S(1)} %get-tuple-element.50.u0), channel_id=1, source_target_pairs={{0,24},{8,0},{16,8},{24,16},{1,25},{9,1},{17,9},{25,17},{2,26},{10... | collective-permute-start | bytes 344072 | tf_op jit(solution)/shard_map/ppermute | solution.py:27
  103.4 3.4 %collective-permute-done.14.u1 = bf16[2,224,128]{2,1,0:T(8,128)(2,1)S(1)} collective-permute-done((bf16[2,224,128]{2,1,0:T(8,128)(2,1)S(1)}, bf16[2,224,128]{2,1,0:T(8,128)(2,1)S(1)}, u32[]{:S(2)}, u32[]{:S(2)}) %collective-permute-start.14) | collective-permute-done | bytes 114720 | tf_op jit(solution)/shard_map/ppermute | solution.py:27
  107.5 2.4 %back.2 = bf16[8,224,128]{2,1,0:T(8,128)(2,1)S(1)} custom-call(s32[4]{0:T(128)S(1)} %pad_add_fusion.at_ref, bf16[2,8,128,512]{3,2,1,0:T(8,128)(2,1)S(1)} %get-tuple-element.36.basis_ref, bf16[8,2,224,128]{3,2,1,0:T(8,128)(2,1)S(1)} %all-to-all-done.2.w_ref, bf16[2,224,128]{2,1,0:T(8,128)(2,1)S(1)} %get-tuple-element.50.u0, ...), custom_call_target="tpu_custom_call" | custom-call | flops 234881024 | bytes 3145728 | tf_op jit(solution)/shard_map/back/pallas_call | solution.py:293
  109.9 16.7 %all_to_all.25 = bf16[8,224,128]{2,1,0:T(8,128)(2,1)} all-to-all(bf16[8,224,128]{2,1,0:T(8,128)(2,1)S(1)} %back.2), channel_id=1, replica_groups=mesh['x'=4,'core'=2,'y'=4,'z'=8] {'z'}, dimensions={0} | all-to-all | bytes 917504 | tf_op jit(solution)/shard_map/all_to_all | solution.py:31
  127.8 1.4 collective-permute-start.17
  129.2 1.4 collective-permute-start.19
  135.6 6.1 %collective-permute-start.25 = (bf16[128,1792]{1,0:T(8,128)(2,1)S(1)}, bf16[128,1792]{1,0:T(8,128)(2,1)S(1)}, u32[]{:S(2)}, u32[]{:S(2)}) collective-permute-start(bf16[128,1792]{1,0:T(8,128)(2,1)S(1)} %bitcast.12), channel_id=1, source_target_pairs={{0,32},{32,0},{1,33},{33,1},{2,34},{34,2},{3,35},{35,3},{4,36},{36... | collective-permute-start | bytes 1376264 | tf_op jit(solution)/shard_map/ppermute | solution.py:27
  141.6 1.4 collective-permute-start.23
  144.2 7.5 %collective-permute-done.27.refs_2_ = bf16[224,128]{1,0:T(8,128)(2,1)S(1)} collective-permute-done((bf16[224,128]{1,0:T(8,128)(2,1)S(1)}, bf16[224,128]{1,0:T(8,128)(2,1)S(1)}, u32[]{:S(2)}, u32[]{:S(2)}) %collective-permute-start.27) | collective-permute-done | bytes 57376 | tf_op jit(solution)/shard_map/ppermute | solution.py:27
  151.8 3.3 %collective-permute-start.30 = (bf16[224,128]{1,0:T(8,128)(2,1)S(1)}, bf16[224,128]{1,0:T(8,128)(2,1)S(1)}, u32[]{:S(2)}, u32[]{:S(2)}) collective-permute-start(bf16[224,128]{1,0:T(8,128)(2,1)S(1)} %get-tuple-element.56), channel_id=1, source_target_pairs={{0,5},{1,6},{2,7},{3,0},{4,1},{5,2},{6,3},{7,4},{8,13},{9,14},{10,... | collective-permute-start | bytes 172040 | tf_op jit(solution)/shard_map/ppermute | solution.py:27
  155.1 4.2 %collective-permute-done.29.refs_4_ = bf16[224,128]{1,0:T(8,128)(2,1)S(1)} collective-permute-done((bf16[224,128]{1,0:T(8,128)(2,1)S(1)}, bf16[224,128]{1,0:T(8,128)(2,1)S(1)}, u32[]{:S(2)}, u32[]{:S(2)}) %collective-permute-start.29) | collective-permute-done | bytes 57376 | tf_op jit(solution)/shard_map/ppermute | solution.py:27
  160.6 2.1 %collective-permute-start.24 = (bf16[128,1792]{1,0:T(8,128)(2,1)}, bf16[128,1792]{1,0:T(8,128)(2,1)S(1)}, u32[]{:S(2)}, u32[]{:S(2)}) collective-permute-start(bf16[128,1792]{1,0:T(8,128)(2,1)} %collective-permute-done.19.refs_1_), channel_id=1, source_target_pairs={{0,32},{32,0},{1,33},{33,1},{2,34},{34,2},{3,35},{35,3},{4,36},{36... | collective-permute-start | bytes 1376264 | tf_op jit(solution)/shard_map/ppermute | solution.py:27
  162.7 1.6 slice.16
  164.4 1.6 slice.17
  166.3 2.4 %collective-permute-start.20 = (bf16[64,1792]{1,0:T(8,128)(2,1)}, bf16[64,1792]{1,0:T(8,128)(2,1)S(1)}, u32[]{:S(2)}, u32[]{:S(2)}) collective-permute-start(bf16[64,1792]{1,0:T(8,128)(2,1)} %slice.17), channel_id=1, source_target_pairs={{0,192},{64,0},{128,64},{192,128},{1,193},{65,1},{129,65},{193,129... | collective-permute-start | bytes 688136 | tf_op jit(solution)/shard_map/ppermute | solution.py:27
  169.5 5.4 %all-to-all-start.4 = ((f32[8,64,224]{2,1,0:T(8,128)}), f32[8,64,224]{2,1,0:T(8,128)S(1)}, u32[]{:S(2)}, u32[]{:S(2)}) async-start(f32[8,64,224]{2,1,0:T(8,128)} %get-tuple-element.66), calls=%async_computation.4 | async-start | bytes 1048576 | tf_op jit(solution)/shard_map/all_to_all | solution.py:31
  175.0 2.7 %collective-permute-start.34 = (bf16[128,1792]{1,0:T(8,128)(2,1)S(1)}, bf16[128,1792]{1,0:T(8,128)(2,1)S(1)}, u32[]{:S(2)}, u32[]{:S(2)}) collective-permute-start(bf16[128,1792]{1,0:T(8,128)(2,1)S(1)} %turn.1.refs_0_), channel_id=1, source_target_pairs={{0,192},{64,0},{128,64},{192,128},{1,193},{65,1},{129,65},{193,129... | collective-permute-start | bytes 1376264 | tf_op jit(solution)/shard_map/ppermute | solution.py:27
  177.7 1.4 collective-permute-start.21
  179.2 1.5 place.6.refs_4_
  181.2 2.4 %place.7.refs_4_ = bf16[2,128,14336]{2,1,0:T(8,128)(2,1)} custom-call(s32[4]{0:T(128)S(1)} %pad_add_fusion.at_ref, bf16[128,1792]{1,0:T(8,128)(2,1)} %collective-permute-done.17.refs_0_, bf16[128,1792]{1,0:T(8,128)(2,1)} %collective-permute-done.19.refs_1_, bf16[128,1792]{1,0:T(8,128)(2,1)S(1)} %collective-permute-done.23.refs_2_, ...), custom_call_target="tpu_custom_call", output_to_operand_aliasing={{}: (5, {})} | custom-call | flops 2000000000 | bytes 3670016 | tf_op jit(solution)/shard_map/place/pallas_call | solution.py:354
  183.6 1.5 place.8.refs_2_
  185.1 2.3 %collective-permute-done.33.refs_0_ = bf16[128,1792]{1,0:T(8,128)(2,1)S(1)} collective-permute-done((bf16[128,1792]{1,0:T(8,128)(2,1)S(1)}, bf16[128,1792]{1,0:T(8,128)(2,1)S(1)}, u32[]{:S(2)}, u32[]{:S(2)}) %collective-permute-start.33) | collective-permute-done | bytes 458784 | tf_op jit(solution)/shard_map/ppermute | solution.py:27
  187.4 1.7 collective-permute-start.35
  189.3 2.8 %collective-permute-start.39 = (bf16[64,1792]{1,0:T(8,128)(2,1)S(1)}, bf16[64,1792]{1,0:T(8,128)(2,1)S(1)}, u32[]{:S(2)}, u32[]{:S(2)}) collective-permute-start(bf16[64,1792]{1,0:T(8,128)(2,1)S(1)} %slice.15), channel_id=1, source_target_pairs={{0,192},{64,0},{128,64},{192,128},{1,193},{65,1},{129,65},{193,129... | collective-permute-start | bytes 688136 | tf_op jit(solution)/shard_map/ppermute | solution.py:27
  192.0 1.5 place.9.refs_4_
  193.5 1.8 place.10.refs_4_
  195.3 1.8 collective-permute-done.38.refs_0_
  200.0 1.5 place.11
  (107 shorter events, 28.1 us)
Async XLA Ops:
  2.8 10.4 %copy-start.14 = (bf16[2,128,1792]{2,1,0:T(8,128)(2,1)S(1)}, bf16[2,128,1792]{2,1,0:T(8,128)(2,1)}, u32[]{:S(2)}) copy-start(bf16[2,128,1792]{2,1,0:T(8,128)(2,1)} %v_ref.4) | copy-start | bytes 2752516
  4.3 20.3 %all-to-all-start.1 = ((bf16[8,144,128]{2,1,0:T(8,128)(2,1)}), bf16[8,144,128]{2,1,0:T(8,128)(2,1)S(1)}, u32[]{:S(2)}, u32[]{:S(2)}) async-start(bf16[8,144,128]{2,1,0:T(8,128)(2,1)} %pieces.1), calls=%async_computation.1 | async-start | bytes 589824 | tf_op jit(solution)/shard_map/all_to_all | solution.py:31
  24.5 28.2 %all-to-all-start = ((bf16[8,2,224,128]{3,2,1,0:T(8,128)(2,1)}), bf16[8,2,224,128]{3,2,1,0:T(8,128)(2,1)S(1)}, u32[]{:S(2)}, u32[]{:S(2)}) async-start(bf16[8,2,224,128]{3,2,1,0:T(8,128)(2,1)} %pack.2), calls=%async_computation | async-start | bytes 1835008 | tf_op jit(solution)/shard_map/all_to_all | solution.py:31
  28.1 7.6 %collective-permute-start = (bf16[8,144,128]{2,1,0:T(8,128)(2,1)S(1)}, bf16[8,144,128]{2,1,0:T(8,128)(2,1)S(1)}, u32[]{:S(2)}, u32[]{:S(2)}) collective-permute-start(bf16[8,144,128]{2,1,0:T(8,128)(2,1)S(1)} %all-to-all-done.1), channel_id=1, source_target_pairs={{0,64},{64,128},{128,192},{192,0},{1,65},{65,129},{129,193},{193,1... | collective-permute-start | bytes 884744 | tf_op jit(solution)/shard_map/ppermute | solution.py:27
  29.4 13.6 %collective-permute-start.1 = (bf16[8,144,128]{2,1,0:T(8,128)(2,1)S(1)}, bf16[8,144,128]{2,1,0:T(8,128)(2,1)S(1)}, u32[]{:S(2)}, u32[]{:S(2)}) collective-permute-start(bf16[8,144,128]{2,1,0:T(8,128)(2,1)S(1)} %all-to-all-done.1), channel_id=1, source_target_pairs={{0,128},{64,192},{128,0},{192,64},{1,129},{65,193},{129,1},{193,65... | collective-permute-start | bytes 884744 | tf_op jit(solution)/shard_map/ppermute | solution.py:27
  31.8 11.5 %collective-permute-start.2 = (bf16[8,144,128]{2,1,0:T(8,128)(2,1)S(1)}, bf16[8,144,128]{2,1,0:T(8,128)(2,1)S(1)}, u32[]{:S(2)}, u32[]{:S(2)}) collective-permute-start(bf16[8,144,128]{2,1,0:T(8,128)(2,1)S(1)} %all-to-all-done.1), channel_id=1, source_target_pairs={{0,192},{64,0},{128,64},{192,128},{1,193},{65,1},{129,65},{193,129... | collective-permute-start | bytes 884744 | tf_op jit(solution)/shard_map/ppermute | solution.py:27
  43.5 12.8 %collective-permute-start.3 = (bf16[4,8,144,128]{3,2,1,0:T(8,128)(2,1)S(1)}, bf16[4,8,144,128]{3,2,1,0:T(8,128)(2,1)}, u32[]{:S(2)}, u32[]{:S(2)}) collective-permute-start(bf16[4,8,144,128]{3,2,1,0:T(8,128)(2,1)S(1)} %pad_maximum_fusion.own_ref), channel_id=1, source_target_pairs={{0,32},{32,0},{1,33},{33,1},{2,34},{34,2},{3,35},{35,3},{4,36},{36... | collective-permute-start | bytes 3538952 | tf_op jit(solution)/shard_map/ppermute | solution.py:27
  52.8 54.7 %all-to-all-start.2 = ((bf16[8,2,224,128]{3,2,1,0:T(8,128)(2,1)}), bf16[8,2,224,128]{3,2,1,0:T(8,128)(2,1)S(1)}, u32[]{:S(2)}, u32[]{:S(2)}) async-start(bf16[8,2,224,128]{3,2,1,0:T(8,128)(2,1)} %copy-done.4), calls=%async_computation.2 | async-start | bytes 1835008 | tf_op jit(solution)/shard_map/all_to_all | solution.py:31
  61.6 25.2 %collective-permute-start.4 = (f32[2,232,128]{2,1,0:T(8,128)S(1)}, f32[2,232,128]{2,1,0:T(8,128)S(1)}, u32[]{:S(2)}, u32[]{:S(2)}) collective-permute-start(f32[2,232,128]{2,1,0:T(8,128)S(1)} %get-tuple-element.39), channel_id=1, source_target_pairs={{0,8},{8,16},{16,24},{24,0},{1,9},{9,17},{17,25},{25,1},{2,10},{10... | collective-permute-start | bytes 712712 | tf_op jit(solution)/shard_map/ppermute | solution.py:27
  62.9 26.7 %collective-permute-start.5 = (f32[2,232,128]{2,1,0:T(8,128)S(1)}, f32[2,232,128]{2,1,0:T(8,128)S(1)}, u32[]{:S(2)}, u32[]{:S(2)}) collective-permute-start(f32[2,232,128]{2,1,0:T(8,128)S(1)} %get-tuple-element.40), channel_id=1, source_target_pairs={{0,16},{8,24},{16,0},{24,8},{1,17},{9,25},{17,1},{25,9},{2,18},{10... | collective-permute-start | bytes 712712 | tf_op jit(solution)/shard_map/ppermute | solution.py:27
  65.5 25.3 %collective-permute-start.6 = (f32[2,232,128]{2,1,0:T(8,128)S(1)}, f32[2,232,128]{2,1,0:T(8,128)S(1)}, u32[]{:S(2)}, u32[]{:S(2)}) collective-permute-start(f32[2,232,128]{2,1,0:T(8,128)S(1)} %get-tuple-element.41), channel_id=1, source_target_pairs={{0,24},{8,0},{16,8},{24,16},{1,25},{9,1},{17,9},{25,17},{2,26},{10... | collective-permute-start | bytes 712712 | tf_op jit(solution)/shard_map/ppermute | solution.py:27
  67.4 16.8 %collective-permute-start.10 = (f32[64,224]{1,0:T(8,128)S(1)}, f32[64,224]{1,0:T(8,128)S(1)}, u32[]{:S(2)}, u32[]{:S(2)}) collective-permute-start(f32[64,224]{1,0:T(8,128)S(1)} %get-tuple-element.46), channel_id=1, source_target_pairs={{0,4},{1,5},{2,6},{3,7},{4,0},{5,1},{6,2},{7,3},{8,12},{9,13},{10,... | collective-permute-start | bytes 172040 | tf_op jit(solution)/shard_map/ppermute | solution.py:27
  72.8 11.5 %collective-permute-start.11 = (f32[64,224]{1,0:T(8,128)S(1)}, f32[64,224]{1,0:T(8,128)S(1)}, u32[]{:S(2)}, u32[]{:S(2)}) collective-permute-start(f32[64,224]{1,0:T(8,128)S(1)} %get-tuple-element.47), channel_id=1, source_target_pairs={{0,5},{1,6},{2,7},{3,0},{4,1},{5,2},{6,3},{7,4},{8,13},{9,14},{10,... | collective-permute-start | bytes 172040 | tf_op jit(solution)/shard_map/ppermute | solution.py:27
  84.2 6.7 %collective-permute-start.12 = (f32[64,224]{1,0:T(8,128)S(1)}, f32[64,224]{1,0:T(8,128)S(1)}, u32[]{:S(2)}, u32[]{:S(2)}) collective-permute-start(f32[64,224]{1,0:T(8,128)S(1)} %get-tuple-element.48), channel_id=1, source_target_pairs={{0,6},{1,7},{2,0},{3,1},{4,2},{5,3},{6,4},{7,5},{8,14},{9,15},{10,... | collective-permute-start | bytes 172040 | tf_op jit(solution)/shard_map/ppermute | solution.py:27
  84.2 7.3 %collective-permute-start.13 = (f32[64,224]{1,0:T(8,128)S(1)}, f32[64,224]{1,0:T(8,128)S(1)}, u32[]{:S(2)}, u32[]{:S(2)}) collective-permute-start(f32[64,224]{1,0:T(8,128)S(1)} %get-tuple-element.49), channel_id=1, source_target_pairs={{0,7},{1,0},{2,1},{3,2},{4,3},{5,4},{6,5},{7,6},{8,15},{9,8},{10,9... | collective-permute-start | bytes 172040 | tf_op jit(solution)/shard_map/ppermute | solution.py:27
  86.8 4.7 %collective-permute-start.7 = (f32[64,224]{1,0:T(8,128)S(1)}, f32[64,224]{1,0:T(8,128)S(1)}, u32[]{:S(2)}, u32[]{:S(2)}) collective-permute-start(f32[64,224]{1,0:T(8,128)S(1)} %get-tuple-element.43), channel_id=1, source_target_pairs={{0,1},{1,2},{2,3},{3,4},{4,5},{5,6},{6,7},{7,0},{8,9},{9,10},{10,1... | collective-permute-start | bytes 172040 | tf_op jit(solution)/shard_map/ppermute | solution.py:27
  89.6 5.7 %collective-permute-start.8 = (f32[64,224]{1,0:T(8,128)S(1)}, f32[64,224]{1,0:T(8,128)S(1)}, u32[]{:S(2)}, u32[]{:S(2)}) collective-permute-start(f32[64,224]{1,0:T(8,128)S(1)} %get-tuple-element.44), channel_id=1, source_target_pairs={{0,2},{1,3},{2,4},{3,5},{4,6},{5,7},{6,0},{7,1},{8,10},{9,11},{10,... | collective-permute-start | bytes 172040 | tf_op jit(solution)/shard_map/ppermute | solution.py:27
  90.9 8.3 %collective-permute-start.9 = (f32[64,224]{1,0:T(8,128)S(1)}, f32[64,224]{1,0:T(8,128)S(1)}, u32[]{:S(2)}, u32[]{:S(2)}) collective-permute-start(f32[64,224]{1,0:T(8,128)S(1)} %get-tuple-element.45), channel_id=1, source_target_pairs={{0,3},{1,4},{2,5},{3,6},{4,7},{5,0},{6,1},{7,2},{8,11},{9,12},{10,... | collective-permute-start | bytes 172040 | tf_op jit(solution)/shard_map/ppermute | solution.py:27
  100.8 9.1 %copy-start.5 = (bf16[2,224,128]{2,1,0:T(8,128)(2,1)}, bf16[2,224,128]{2,1,0:T(8,128)(2,1)S(1)}, u32[]{:S(2)}) copy-start(bf16[2,224,128]{2,1,0:T(8,128)(2,1)S(1)} %get-tuple-element.50.u0) | copy-start | bytes 344068
  100.8 6.1 %collective-permute-start.14 = (bf16[2,224,128]{2,1,0:T(8,128)(2,1)S(1)}, bf16[2,224,128]{2,1,0:T(8,128)(2,1)S(1)}, u32[]{:S(2)}, u32[]{:S(2)}) collective-permute-start(bf16[2,224,128]{2,1,0:T(8,128)(2,1)S(1)} %get-tuple-element.50.u0), channel_id=1, source_target_pairs={{0,8},{8,16},{16,24},{24,0},{1,9},{9,17},{17,25},{25,1},{2,10},{10... | collective-permute-start | bytes 344072 | tf_op jit(solution)/shard_map/ppermute | solution.py:27
  100.8 6.1 %collective-permute-start.15 = (bf16[2,224,128]{2,1,0:T(8,128)(2,1)S(1)}, bf16[2,224,128]{2,1,0:T(8,128)(2,1)S(1)}, u32[]{:S(2)}, u32[]{:S(2)}) collective-permute-start(bf16[2,224,128]{2,1,0:T(8,128)(2,1)S(1)} %get-tuple-element.50.u0), channel_id=1, source_target_pairs={{0,16},{8,24},{16,0},{24,8},{1,17},{9,25},{17,1},{25,9},{2,18},{10... | collective-permute-start | bytes 344072 | tf_op jit(solution)/shard_map/ppermute | solution.py:27
  100.8 6.7 %collective-permute-start.16 = (bf16[2,224,128]{2,1,0:T(8,128)(2,1)S(1)}, bf16[2,224,128]{2,1,0:T(8,128)(2,1)S(1)}, u32[]{:S(2)}, u32[]{:S(2)}) collective-permute-start(bf16[2,224,128]{2,1,0:T(8,128)(2,1)S(1)} %get-tuple-element.50.u0), channel_id=1, source_target_pairs={{0,24},{8,0},{16,8},{24,16},{1,25},{9,1},{17,9},{25,17},{2,26},{10... | collective-permute-start | bytes 344072 | tf_op jit(solution)/shard_map/ppermute | solution.py:27
  127.8 13.8 %collective-permute-start.17 = (bf16[128,1792]{1,0:T(8,128)(2,1)S(1)}, bf16[128,1792]{1,0:T(8,128)(2,1)}, u32[]{:S(2)}, u32[]{:S(2)}) collective-permute-start(bf16[128,1792]{1,0:T(8,128)(2,1)S(1)} %bitcast.10), channel_id=1, source_target_pairs={{0,64},{64,128},{128,192},{192,0},{1,65},{65,129},{129,193},{193,1... | collective-permute-start | bytes 1376264 | tf_op jit(solution)/shard_map/ppermute | solution.py:27
  129.2 31.4 %collective-permute-start.19 = (bf16[128,1792]{1,0:T(8,128)(2,1)S(1)}, bf16[128,1792]{1,0:T(8,128)(2,1)}, u32[]{:S(2)}, u32[]{:S(2)}) collective-permute-start(bf16[128,1792]{1,0:T(8,128)(2,1)S(1)} %bitcast.11), channel_id=1, source_target_pairs={{0,192},{64,0},{128,64},{192,128},{1,193},{65,1},{129,65},{193,129... | collective-permute-start | bytes 1376264 | tf_op jit(solution)/shard_map/ppermute | solution.py:27
  135.4 7.6 %collective-permute-start.26 = (bf16[224,128]{1,0:T(8,128)(2,1)S(1)}, bf16[224,128]{1,0:T(8,128)(2,1)S(1)}, u32[]{:S(2)}, u32[]{:S(2)}) collective-permute-start(bf16[224,128]{1,0:T(8,128)(2,1)S(1)} %get-tuple-element.52), channel_id=1, source_target_pairs={{0,1},{1,2},{2,3},{3,4},{4,5},{5,6},{6,7},{7,0},{8,9},{9,10},{10,1... | collective-permute-start | bytes 172040 | tf_op jit(solution)/shard_map/ppermute | solution.py:27
  135.6 39.3 %collective-permute-start.25 = (bf16[128,1792]{1,0:T(8,128)(2,1)S(1)}, bf16[128,1792]{1,0:T(8,128)(2,1)S(1)}, u32[]{:S(2)}, u32[]{:S(2)}) collective-permute-start(bf16[128,1792]{1,0:T(8,128)(2,1)S(1)} %bitcast.12), channel_id=1, source_target_pairs={{0,32},{32,0},{1,33},{33,1},{2,34},{34,2},{3,35},{35,3},{4,36},{36... | collective-permute-start | bytes 1376264 | tf_op jit(solution)/shard_map/ppermute | solution.py:27
  141.6 37.4 %collective-permute-start.23 = (bf16[128,1792]{1,0:T(8,128)(2,1)}, bf16[128,1792]{1,0:T(8,128)(2,1)S(1)}, u32[]{:S(2)}, u32[]{:S(2)}) collective-permute-start(bf16[128,1792]{1,0:T(8,128)(2,1)} %collective-permute-done.17.refs_0_), channel_id=1, source_target_pairs={{0,32},{32,0},{1,33},{33,1},{2,34},{34,2},{3,35},{35,3},{4,36},{36... | collective-permute-start | bytes 1376264 | tf_op jit(solution)/shard_map/ppermute | solution.py:27
  143.0 8.7 %collective-permute-start.27 = (bf16[224,128]{1,0:T(8,128)(2,1)S(1)}, bf16[224,128]{1,0:T(8,128)(2,1)S(1)}, u32[]{:S(2)}, u32[]{:S(2)}) collective-permute-start(bf16[224,128]{1,0:T(8,128)(2,1)S(1)} %get-tuple-element.53), channel_id=1, source_target_pairs={{0,2},{1,3},{2,4},{3,5},{4,6},{5,7},{6,0},{7,1},{8,10},{9,11},{10,... | collective-permute-start | bytes 172040 | tf_op jit(solution)/shard_map/ppermute | solution.py:27
  143.0 8.7 %collective-permute-start.28 = (bf16[224,128]{1,0:T(8,128)(2,1)S(1)}, bf16[224,128]{1,0:T(8,128)(2,1)S(1)}, u32[]{:S(2)}, u32[]{:S(2)}) collective-permute-start(bf16[224,128]{1,0:T(8,128)(2,1)S(1)} %get-tuple-element.54), channel_id=1, source_target_pairs={{0,3},{1,4},{2,5},{3,6},{4,7},{5,0},{6,1},{7,2},{8,11},{9,12},{10,... | collective-permute-start | bytes 172040 | tf_op jit(solution)/shard_map/ppermute | solution.py:27
  151.8 7.5 %collective-permute-start.29 = (bf16[224,128]{1,0:T(8,128)(2,1)S(1)}, bf16[224,128]{1,0:T(8,128)(2,1)S(1)}, u32[]{:S(2)}, u32[]{:S(2)}) collective-permute-start(bf16[224,128]{1,0:T(8,128)(2,1)S(1)} %get-tuple-element.55), channel_id=1, source_target_pairs={{0,4},{1,5},{2,6},{3,7},{4,0},{5,1},{6,2},{7,3},{8,12},{9,13},{10,... | collective-permute-start | bytes 172040 | tf_op jit(solution)/shard_map/ppermute | solution.py:27
  151.8 7.5 %collective-permute-start.30 = (bf16[224,128]{1,0:T(8,128)(2,1)S(1)}, bf16[224,128]{1,0:T(8,128)(2,1)S(1)}, u32[]{:S(2)}, u32[]{:S(2)}) collective-permute-start(bf16[224,128]{1,0:T(8,128)(2,1)S(1)} %get-tuple-element.56), channel_id=1, source_target_pairs={{0,5},{1,6},{2,7},{3,0},{4,1},{5,2},{6,3},{7,4},{8,13},{9,14},{10,... | collective-permute-start | bytes 172040 | tf_op jit(solution)/shard_map/ppermute | solution.py:27
  159.3 6.7 %collective-permute-start.31 = (bf16[224,128]{1,0:T(8,128)(2,1)S(1)}, bf16[224,128]{1,0:T(8,128)(2,1)S(1)}, u32[]{:S(2)}, u32[]{:S(2)}) collective-permute-start(bf16[224,128]{1,0:T(8,128)(2,1)S(1)} %get-tuple-element.57), channel_id=1, source_target_pairs={{0,6},{1,7},{2,0},{3,1},{4,2},{5,3},{6,4},{7,5},{8,14},{9,15},{10,... | collective-permute-start | bytes 172040 | tf_op jit(solution)/shard_map/ppermute | solution.py:27
  159.3 7.0 %collective-permute-start.32 = (bf16[224,128]{1,0:T(8,128)(2,1)S(1)}, bf16[224,128]{1,0:T(8,128)(2,1)S(1)}, u32[]{:S(2)}, u32[]{:S(2)}) collective-permute-start(bf16[224,128]{1,0:T(8,128)(2,1)S(1)} %get-tuple-element.58), channel_id=1, source_target_pairs={{0,7},{1,0},{2,1},{3,2},{4,3},{5,4},{6,5},{7,6},{8,15},{9,8},{10,9... | collective-permute-start | bytes 172040 | tf_op jit(solution)/shard_map/ppermute | solution.py:27
  160.6 20.0 %collective-permute-start.24 = (bf16[128,1792]{1,0:T(8,128)(2,1)}, bf16[128,1792]{1,0:T(8,128)(2,1)S(1)}, u32[]{:S(2)}, u32[]{:S(2)}) collective-permute-start(bf16[128,1792]{1,0:T(8,128)(2,1)} %collective-permute-done.19.refs_1_), channel_id=1, source_target_pairs={{0,32},{32,0},{1,33},{33,1},{2,34},{34,2},{3,35},{35,3},{4,36},{36... | collective-permute-start | bytes 1376264 | tf_op jit(solution)/shard_map/ppermute | solution.py:27
  166.0 9.0 %collective-permute-start.18 = (bf16[64,1792]{1,0:T(8,128)(2,1)}, bf16[64,1792]{1,0:T(8,128)(2,1)S(1)}, u32[]{:S(2)}, u32[]{:S(2)}) collective-permute-start(bf16[64,1792]{1,0:T(8,128)(2,1)} %slice.16), channel_id=1, source_target_pairs={{0,64},{64,128},{128,192},{192,0},{1,65},{65,129},{129,193},{193,1... | collective-permute-start | bytes 688136 | tf_op jit(solution)/shard_map/ppermute | solution.py:27
  166.3 11.4 %collective-permute-start.20 = (bf16[64,1792]{1,0:T(8,128)(2,1)}, bf16[64,1792]{1,0:T(8,128)(2,1)S(1)}, u32[]{:S(2)}, u32[]{:S(2)}) collective-permute-start(bf16[64,1792]{1,0:T(8,128)(2,1)} %slice.17), channel_id=1, source_target_pairs={{0,192},{64,0},{128,64},{192,128},{1,193},{65,1},{129,65},{193,129... | collective-permute-start | bytes 688136 | tf_op jit(solution)/shard_map/ppermute | solution.py:27
  169.5 29.0 %all-to-all-start.4 = ((f32[8,64,224]{2,1,0:T(8,128)}), f32[8,64,224]{2,1,0:T(8,128)S(1)}, u32[]{:S(2)}, u32[]{:S(2)}) async-start(f32[8,64,224]{2,1,0:T(8,128)} %get-tuple-element.66), calls=%async_computation.4 | async-start | bytes 1048576 | tf_op jit(solution)/shard_map/all_to_all | solution.py:31
  174.9 12.5 %collective-permute-start.33 = (bf16[128,1792]{1,0:T(8,128)(2,1)S(1)}, bf16[128,1792]{1,0:T(8,128)(2,1)S(1)}, u32[]{:S(2)}, u32[]{:S(2)}) collective-permute-start(bf16[128,1792]{1,0:T(8,128)(2,1)S(1)} %turn.1.refs_0_), channel_id=1, source_target_pairs={{0,64},{64,128},{128,192},{192,0},{1,65},{65,129},{129,193},{193,1... | collective-permute-start | bytes 1376264 | tf_op jit(solution)/shard_map/ppermute | solution.py:27
  175.0 12.4 %collective-permute-start.34 = (bf16[128,1792]{1,0:T(8,128)(2,1)S(1)}, bf16[128,1792]{1,0:T(8,128)(2,1)S(1)}, u32[]{:S(2)}, u32[]{:S(2)}) collective-permute-start(bf16[128,1792]{1,0:T(8,128)(2,1)S(1)} %turn.1.refs_0_), channel_id=1, source_target_pairs={{0,192},{64,0},{128,64},{192,128},{1,193},{65,1},{129,65},{193,129... | collective-permute-start | bytes 1376264 | tf_op jit(solution)/shard_map/ppermute | solution.py:27
  177.7 5.9 %collective-permute-start.21 = (bf16[64,1792]{1,0:T(8,128)(2,1)S(1)}, bf16[64,1792]{1,0:T(8,128)(2,1)S(1)}, u32[]{:S(2)}, u32[]{:S(2)}) collective-permute-start(bf16[64,1792]{1,0:T(8,128)(2,1)S(1)} %collective-permute-done.18.refs_0_), channel_id=1, source_target_pairs={{0,32},{32,0},{1,33},{33,1},{2,34},{34,2},{3,35},{35,3},{4,36},{36... | collective-permute-start | bytes 688136 | tf_op jit(solution)/shard_map/ppermute | solution.py:27
  179.1 4.5 %collective-permute-start.22 = (bf16[64,1792]{1,0:T(8,128)(2,1)S(1)}, bf16[64,1792]{1,0:T(8,128)(2,1)S(1)}, u32[]{:S(2)}, u32[]{:S(2)}) collective-permute-start(bf16[64,1792]{1,0:T(8,128)(2,1)S(1)} %collective-permute-done.20.refs_1_), channel_id=1, source_target_pairs={{0,32},{32,0},{1,33},{33,1},{2,34},{34,2},{3,35},{35,3},{4,36},{36... | collective-permute-start | bytes 688136 | tf_op jit(solution)/shard_map/ppermute | solution.py:27
  180.7 11.4 %collective-permute-start.37 = (bf16[128,1792]{1,0:T(8,128)(2,1)S(1)}, bf16[128,1792]{1,0:T(8,128)(2,1)S(1)}, u32[]{:S(2)}, u32[]{:S(2)}) collective-permute-start(bf16[128,1792]{1,0:T(8,128)(2,1)S(1)} %turn.1.refs_0_), channel_id=1, source_target_pairs={{0,32},{32,0},{1,33},{33,1},{2,34},{34,2},{3,35},{35,3},{4,36},{36... | collective-permute-start | bytes 1376264 | tf_op jit(solution)/shard_map/ppermute | solution.py:27
  187.4 6.1 %collective-permute-start.35 = (bf16[128,1792]{1,0:T(8,128)(2,1)S(1)}, bf16[128,1792]{1,0:T(8,128)(2,1)S(1)}, u32[]{:S(2)}, u32[]{:S(2)}) collective-permute-start(bf16[128,1792]{1,0:T(8,128)(2,1)S(1)} %collective-permute-done.33.refs_0_), channel_id=1, source_target_pairs={{0,32},{32,0},{1,33},{33,1},{2,34},{34,2},{3,35},{35,3},{4,36},{36... | collective-permute-start | bytes 1376264 | tf_op jit(solution)/shard_map/ppermute | solution.py:27
  189.1 4.4 %collective-permute-start.36 = (bf16[128,1792]{1,0:T(8,128)(2,1)S(1)}, bf16[128,1792]{1,0:T(8,128)(2,1)S(1)}, u32[]{:S(2)}, u32[]{:S(2)}) collective-permute-start(bf16[128,1792]{1,0:T(8,128)(2,1)S(1)} %collective-permute-done.34.refs_1_), channel_id=1, source_target_pairs={{0,32},{32,0},{1,33},{33,1},{2,34},{34,2},{3,35},{35,3},{4,36},{36... | collective-permute-start | bytes 1376264 | tf_op jit(solution)/shard_map/ppermute | solution.py:27
  189.2 8.0 %collective-permute-start.38 = (bf16[64,1792]{1,0:T(8,128)(2,1)S(1)}, bf16[64,1792]{1,0:T(8,128)(2,1)S(1)}, u32[]{:S(2)}, u32[]{:S(2)}) collective-permute-start(bf16[64,1792]{1,0:T(8,128)(2,1)S(1)} %slice.14), channel_id=1, source_target_pairs={{0,64},{64,128},{128,192},{192,0},{1,65},{65,129},{129,193},{193,1... | collective-permute-start | bytes 688136 | tf_op jit(solution)/shard_map/ppermute | solution.py:27
  189.3 7.9 %collective-permute-start.39 = (bf16[64,1792]{1,0:T(8,128)(2,1)S(1)}, bf16[64,1792]{1,0:T(8,128)(2,1)S(1)}, u32[]{:S(2)}, u32[]{:S(2)}) collective-permute-start(bf16[64,1792]{1,0:T(8,128)(2,1)S(1)} %slice.15), channel_id=1, source_target_pairs={{0,192},{64,0},{128,64},{192,128},{1,193},{65,1},{129,65},{193,129... | collective-permute-start | bytes 688136 | tf_op jit(solution)/shard_map/ppermute | solution.py:27
  197.1 2.5 %collective-permute-start.40 = (bf16[64,1792]{1,0:T(8,128)(2,1)S(1)}, bf16[64,1792]{1,0:T(8,128)(2,1)S(1)}, u32[]{:S(2)}, u32[]{:S(2)}) collective-permute-start(bf16[64,1792]{1,0:T(8,128)(2,1)S(1)} %collective-permute-done.38.refs_0_), channel_id=1, source_target_pairs={{0,32},{32,0},{1,33},{33,1},{2,34},{34,2},{3,35},{35,3},{4,36},{36... | collective-permute-start | bytes 688136 | tf_op jit(solution)/shard_map/ppermute | solution.py:27
  198.5 1.5 collective-permute-start.41
  (17 other events, 43.0 us)
where the time goes:
time: 203 us; the launch traced here: 202 us
  starting transfers between devices  80.9 us (40%)
  waiting for transfers between devices  65.5 us (32%)
  Pallas kernels  23.5 us (12%)
  blocking collectives  16.7 us (8%)
  local copies, waits for them, and re-layouts  13.7 us (7%)
    ppermute x42, starting transfers between devices, shift(): return lax.ppermute(v, axis, [(i, (i + k) % n) for i in range(n)])  59.4 us
    ppermute x42, waiting for transfers between devices, shift(): return lax.ppermute(v, axis, [(i, (i + k) % n) for i in range(n)])  50.3 us
    all_to_all x4, starting transfers between devices, exchange(): return lax.all_to_all(v, axis, split_axis=0, concat_axis=0, tiled=True)  21.5 us
    all_to_all x1, blocking collectives, exchange(): return lax.all_to_all(v, axis, split_axis=0, concat_axis=0, tiled=True)  16.7 us
    all_to_all x4, waiting for transfers between devices, exchange(): return lax.all_to_all(v, axis, split_axis=0, concat_axis=0, tiled=True)  15.2 us
    pallas_call x6, Pallas kernels, place(): pl.pallas_call(functools.partial(place_kernel, m, spots), out_shape=jax.S...  10.2 us
    unnamed x38, local copies, waits for them, and re-layouts  9.12 us
  transfers between devices with their start and end apart: 46, of which 17 were waited for; matrix products, arithmetic and copies ran while one was open for 2% of the time, Pallas kernels for 9%

commit v1 on v0

--- a/solution.py
+++ b/solution.py
@@ -390,8 +390,11 @@
     whole_block = back(0, at, gathered, w, updates, False)[0]
     whole_block = exchange(whole_block, "z")
     blocks = back(1, at, gathered, w, updates, True)
-    blocks = [blocks[0]] + [shift(blocks[k], "z", k) for k in range(1, nz)]
-    fresh = [jnp.swapaxes(whole_block.reshape(cols, rows), 0, 1), turn(at, blocks)]
+    moved = [blocks[0]]
+    for k in range(1, nz):
+        moved.append(shift(blocks[k], "z", k))
+    turned = turn(at, moved)
+    fresh = [jnp.swapaxes(whole_block.reshape(cols, rows), 0, 1), turned]
     news = exchange(before(whole_block, news), "z")
     news = unpack_state(news)
 
@@ -406,18 +409,24 @@
     near = []
     for f in fresh:
         near.append((shift(f, "x", 1), shift(f, "x", -1)))
-    whole = put(None, 0, [(fresh[0], 0, 0)])
-    whole = put(whole, 0, [(near[0][0], 3, 0), (near[0][1], 1, 0)])
-    for m in range(mats):
-        left, right = near[m]
-        if m:
-            whole, left, right = lax.optimization_barrier((whole, left, right))
-            whole = put(whole, m, [(fresh[m], 0, 0)])
-            whole = put(whole, m, [(left, 3, 0), (right, 1, 0)])
-        top, low = shift(left[:half], "x", 1), shift(right[half:], "x", -1)
-        if m:
-            whole, top, low = lax.optimization_barrier((whole, top, low))
-        whole = put(whole, m, [(top, 2, 0), (low, 2, half)])
+
+    def far(left, right):
+        return shift(left[:half], "x", 1), shift(right[half:], "x", -1)
+
+    def put_near(whole, m):
+        whole = put(whole, m, [(fresh[m], 0, 0)])
+        return put(whole, m, [(near[m][0], 3, 0), (near[m][1], 1, 0)])
+
+    def put_far(whole, m, top, low):
+        return put(whole, m, [(top, 2, 0), (low, 2, half)])
+
+    first = far(*near[0])
+    whole = put_near(None, 0)
+    second = far(*near[1])
+    whole = put_far(whole, 0, *first)
+    whole = put_near(whole, 1)
+    whole, *second = lax.optimization_barrier((whole, *second))
+    whole = put_far(whole, 1, *second)
     return (whole, news[0], news[1])
 
 

time: 203 us -> 188 us (0.926)
  blocking collectives: 16.7 us -> 0 us
  starting transfers between devices: 80.9 us -> 97.2 us
  waiting for transfers between devices: 65.5 us -> 51.6 us
  local copies, waits for them, and re-layouts: 13.7 us -> 11 us
  Pallas kernels: 23.5 us -> 25.8 us
    all_to_all x1 -> x0, blocking collectives: 16.7 us -> none  [exchange(): return lax.all_to_all(v, axis, split_axis=0, concat_axis=0, tiled=True)]
    ppermute x42, waiting for transfers between devices: 50.3 us -> 36.4 us  [shift(): return lax.ppermute(v, axis, [(i, (i + k) % n) for i in range(n)])]
    ppermute x42, starting transfers between devices: 59.4 us -> 72.5 us  [shift(): return lax.ppermute(v, axis, [(i, (i + k) % n) for i in range(n)])]
    all_to_all x4 -> x5, starting transfers between devices: 21.5 us -> 24.7 us  [exchange(): return lax.all_to_all(v, axis, split_axis=0, concat_axis=0, tiled=True)]
    unnamed x38 -> x30, local copies, waits for them, and re-layouts: 9.12 us -> 6.96 us
    all_to_all x4 -> x5, waiting for transfers between devices: 15.2 us -> 15.2 us  [exchange(): return lax.all_to_all(v, axis, split_axis=0, concat_axis=0, tiled=True)]
  transfers between devices with their start and end apart: 46 -> 47, of which waited for: 17 -> 15; matrix products, arithmetic and copies ran while one was open for 2% -> 2% of each run, Pallas kernels for 9% -> 11%
where the time goes in v1:
time: 188 us; the launch traced here: 187 us
  starting transfers between devices  97.2 us (52%)
  waiting for transfers between devices  51.6 us (27%)
  Pallas kernels  25.8 us (14%)
  local copies, waits for them, and re-layouts  11 us (6%)
    ppermute x42, starting transfers between devices, shift(): return lax.ppermute(v, axis, [(i, (i + k) % n) for i in range(n)])  72.5 us
    ppermute x42, waiting for transfers between devices, shift(): return lax.ppermute(v, axis, [(i, (i + k) % n) for i in range(n)])  36.4 us
    all_to_all x5, starting transfers between devices, exchange(): return lax.all_to_all(v, axis, split_axis=0, concat_axis=0, tiled=True)  24.7 us
    all_to_all x5, waiting for transfers between devices, exchange(): return lax.all_to_all(v, axis, split_axis=0, concat_axis=0, tiled=True)  15.2 us
    pallas_call x6, Pallas kernels, place(): pl.pallas_call(functools.partial(place_kernel, m, spots), out_shape=jax.S...  11.1 us
    unnamed x30, local copies, waits for them, and re-layouts  6.96 us
    pallas_call x2, Pallas kernels, back(): pl.pallas_call(functools.partial(back_kernel, m), out_shape=[jax.ShapeDty...  5 us
  transfers between devices with their start and end apart: 47, of which 15 were waited for; matrix products, arithmetic and copies ran while one was open for 2% of the time, Pallas kernels for 11%

profile of v1, /device:TPU:1, one launch (start us, length us, event | category | flops | bytes accessed | tf_op | source)
XLA Modules:
  0.0 186.9 jit_solution(7379874925512927432)
XLA Ops:
  2.8 1.4 pieces.1
  4.3 9.0 %all-to-all-start.1 = ((bf16[8,144,128]{2,1,0:T(8,128)(2,1)}), bf16[8,144,128]{2,1,0:T(8,128)(2,1)S(1)}, u32[]{:S(2)}, u32[]{:S(2)}) async-start(bf16[8,144,128]{2,1,0:T(8,128)(2,1)} %pieces.1), calls=%async_computation.1 | async-start | bytes 589824 | tf_op jit(solution)/shard_map/all_to_all | solution.py:31
  14.5 10.0 %all-to-all-done.1 = bf16[8,144,128]{2,1,0:T(8,128)(2,1)S(1)} async-done(((bf16[8,144,128]{2,1,0:T(8,128)(2,1)}), bf16[8,144,128]{2,1,0:T(8,128)(2,1)S(1)}, u32[]{:S(2)}, u32[]{:S(2)}) %all-to-all-start.1) | async-done | bytes 294944 | tf_op jit(solution)/shard_map/all_to_all | solution.py:31
  24.5 3.6 %all-to-all-start = ((bf16[8,2,224,128]{3,2,1,0:T(8,128)(2,1)}), bf16[8,2,224,128]{3,2,1,0:T(8,128)(2,1)S(1)}, u32[]{:S(2)}, u32[]{:S(2)}) async-start(bf16[8,2,224,128]{3,2,1,0:T(8,128)(2,1)} %pack.2), calls=%async_computation | async-start | bytes 1835008 | tf_op jit(solution)/shard_map/all_to_all | solution.py:31
  28.1 1.3 collective-permute-start
  29.4 2.5 %collective-permute-start.1 = (bf16[8,144,128]{2,1,0:T(8,128)(2,1)S(1)}, bf16[8,144,128]{2,1,0:T(8,128)(2,1)S(1)}, u32[]{:S(2)}, u32[]{:S(2)}) collective-permute-start(bf16[8,144,128]{2,1,0:T(8,128)(2,1)S(1)} %all-to-all-done.1), channel_id=1, source_target_pairs={{0,128},{64,192},{128,0},{192,64},{1,129},{65,193},{129,1},{193,65... | collective-permute-start | bytes 884744 | tf_op jit(solution)/shard_map/ppermute | solution.py:27
  33.0 2.7 %collective-permute-done = bf16[8,144,128]{2,1,0:T(8,128)(2,1)S(1)} collective-permute-done((bf16[8,144,128]{2,1,0:T(8,128)(2,1)S(1)}, bf16[8,144,128]{2,1,0:T(8,128)(2,1)S(1)}, u32[]{:S(2)}, u32[]{:S(2)}) %collective-permute-start) | collective-permute-done | bytes 294944 | tf_op jit(solution)/shard_map/ppermute | solution.py:27
  35.7 7.3 %collective-permute-done.1 = bf16[8,144,128]{2,1,0:T(8,128)(2,1)S(1)} collective-permute-done((bf16[8,144,128]{2,1,0:T(8,128)(2,1)S(1)}, bf16[8,144,128]{2,1,0:T(8,128)(2,1)S(1)}, u32[]{:S(2)}, u32[]{:S(2)}) %collective-permute-start.1) | collective-permute-done | bytes 294944 | tf_op jit(solution)/shard_map/ppermute | solution.py:27
  43.5 2.8 %collective-permute-start.3 = (bf16[4,8,144,128]{3,2,1,0:T(8,128)(2,1)S(1)}, bf16[4,8,144,128]{3,2,1,0:T(8,128)(2,1)}, u32[]{:S(2)}, u32[]{:S(2)}) collective-permute-start(bf16[4,8,144,128]{3,2,1,0:T(8,128)(2,1)S(1)} %pad_maximum_fusion.own_ref), channel_id=1, source_target_pairs={{0,32},{32,0},{1,33},{33,1},{2,34},{34,2},{3,35},{35,3},{4,36},{36... | collective-permute-start | bytes 3538952 | tf_op jit(solution)/shard_map/ppermute | solution.py:27
  47.6 5.2 %all-to-all-done.g_ref = bf16[8,2,224,128]{3,2,1,0:T(8,128)(2,1)S(1)} async-done(((bf16[8,2,224,128]{3,2,1,0:T(8,128)(2,1)}), bf16[8,2,224,128]{3,2,1,0:T(8,128)(2,1)S(1)}, u32[]{:S(2)}, u32[]{:S(2)}) %all-to-all-start) | async-done | bytes 917536 | tf_op jit(solution)/shard_map/all_to_all | solution.py:31
  52.8 3.6 %all-to-all-start.2 = ((bf16[8,2,224,128]{3,2,1,0:T(8,128)(2,1)}), bf16[8,2,224,128]{3,2,1,0:T(8,128)(2,1)S(1)}, u32[]{:S(2)}, u32[]{:S(2)}) async-start(bf16[8,2,224,128]{3,2,1,0:T(8,128)(2,1)} %copy-done.4), calls=%async_computation.2 | async-start | bytes 1835008 | tf_op jit(solution)/shard_map/all_to_all | solution.py:31
  58.8 2.8 %project.1 = (bf16[2,8,128,512]{3,2,1,0:T(8,128)(2,1)S(1)}, f32[2,232,128]{2,1,0:T(8,128)S(1)}, f32[2,232,128]{2,1,0:T(8,128)S(1)}, f32[2,232,128]{2,1,0:T(8,128)S(1)}, f32[2,232,128]{2,1,0:T(8,128)S(1)}) custom-call(s32[4]{0:T(128)S(1)} %pad_add_fusion.at_ref, bf16[8,2,224,128]{3,2,1,0:T(8,128)(2,1)S(1)} %copy-done.3, ...), custom_call_target="tpu_custom_call" | custom-call | flops 469762048 | bytes 4194304 | tf_op jit(solution)/shard_map/project/pallas_call | solution.py:202
  61.6 1.4 collective-permute-start.4
  62.9 2.6 %collective-permute-start.5 = (f32[2,232,128]{2,1,0:T(8,128)S(1)}, f32[2,232,128]{2,1,0:T(8,128)S(1)}, u32[]{:S(2)}, u32[]{:S(2)}) collective-permute-start(f32[2,232,128]{2,1,0:T(8,128)S(1)} %get-tuple-element.37), channel_id=1, source_target_pairs={{0,16},{8,24},{16,0},{24,8},{1,17},{9,25},{17,1},{25,9},{2,18},{10... | collective-permute-start | bytes 712712 | tf_op jit(solution)/shard_map/ppermute | solution.py:27
  67.4 5.4 %collective-permute-start.10 = (f32[64,224]{1,0:T(8,128)S(1)}, f32[64,224]{1,0:T(8,128)S(1)}, u32[]{:S(2)}, u32[]{:S(2)}) collective-permute-start(f32[64,224]{1,0:T(8,128)S(1)} %get-tuple-element.43), channel_id=1, source_target_pairs={{0,4},{1,5},{2,6},{3,7},{4,0},{5,1},{6,2},{7,3},{8,12},{9,13},{10,... | collective-permute-start | bytes 172040 | tf_op jit(solution)/shard_map/ppermute | solution.py:27
  73.0 11.2 %collective-permute-done.10.refs_4_ = f32[64,224]{1,0:T(8,128)S(1)} collective-permute-done((f32[64,224]{1,0:T(8,128)S(1)}, f32[64,224]{1,0:T(8,128)S(1)}, u32[]{:S(2)}, u32[]{:S(2)}) %collective-permute-start.10) | collective-permute-done | bytes 57376 | tf_op jit(solution)/shard_map/ppermute | solution.py:27
  84.2 2.5 %collective-permute-start.13 = (f32[64,224]{1,0:T(8,128)S(1)}, f32[64,224]{1,0:T(8,128)S(1)}, u32[]{:S(2)}, u32[]{:S(2)}) collective-permute-start(f32[64,224]{1,0:T(8,128)S(1)} %get-tuple-element.46), channel_id=1, source_target_pairs={{0,7},{1,0},{2,1},{3,2},{4,3},{5,4},{6,5},{7,6},{8,15},{9,8},{10,9... | collective-permute-start | bytes 172040 | tf_op jit(solution)/shard_map/ppermute | solution.py:27
  86.8 2.8 %collective-permute-start.7 = (f32[64,224]{1,0:T(8,128)S(1)}, f32[64,224]{1,0:T(8,128)S(1)}, u32[]{:S(2)}, u32[]{:S(2)}) collective-permute-start(f32[64,224]{1,0:T(8,128)S(1)} %get-tuple-element.40), channel_id=1, source_target_pairs={{0,1},{1,2},{2,3},{3,4},{4,5},{5,6},{6,7},{7,0},{8,9},{9,10},{10,1... | collective-permute-start | bytes 172040 | tf_op jit(solution)/shard_map/ppermute | solution.py:27
  91.5 3.8 %collective-permute-done.8.refs_2_ = f32[64,224]{1,0:T(8,128)S(1)} collective-permute-done((f32[64,224]{1,0:T(8,128)S(1)}, f32[64,224]{1,0:T(8,128)S(1)}, u32[]{:S(2)}, u32[]{:S(2)}) %collective-permute-start.8) | collective-permute-done | bytes 57376 | tf_op jit(solution)/shard_map/ppermute | solution.py:27
  95.3 3.9 %collective-permute-done.9.refs_3_ = f32[64,224]{1,0:T(8,128)S(1)} collective-permute-done((f32[64,224]{1,0:T(8,128)S(1)}, f32[64,224]{1,0:T(8,128)S(1)}, u32[]{:S(2)}, u32[]{:S(2)}) %collective-permute-start.9) | collective-permute-done | bytes 57376 | tf_op jit(solution)/shard_map/ppermute | solution.py:27
  99.2 1.6 moments.1
  100.8 2.7 %collective-permute-start.16 = (bf16[2,224,128]{2,1,0:T(8,128)(2,1)S(1)}, bf16[2,224,128]{2,1,0:T(8,128)(2,1)S(1)}, u32[]{:S(2)}, u32[]{:S(2)}) collective-permute-start(bf16[2,224,128]{2,1,0:T(8,128)(2,1)S(1)} %get-tuple-element.47.u0), channel_id=1, source_target_pairs={{0,24},{8,0},{16,8},{24,16},{1,25},{9,1},{17,9},{25,17},{2,26},{10... | collective-permute-start | bytes 344072 | tf_op jit(solution)/shard_map/ppermute | solution.py:27
  103.4 3.4 %collective-permute-done.14.u1 = bf16[2,224,128]{2,1,0:T(8,128)(2,1)S(1)} collective-permute-done((bf16[2,224,128]{2,1,0:T(8,128)(2,1)S(1)}, bf16[2,224,128]{2,1,0:T(8,128)(2,1)S(1)}, u32[]{:S(2)}, u32[]{:S(2)}) %collective-permute-start.14) | collective-permute-done | bytes 114720 | tf_op jit(solution)/shard_map/ppermute | solution.py:27
  107.5 3.2 %back.3 = bf16[8,224,128]{2,1,0:T(8,128)(2,1)} custom-call(s32[4]{0:T(128)S(1)} %pad_add_fusion.at_ref, bf16[2,8,128,512]{3,2,1,0:T(8,128)(2,1)S(1)} %get-tuple-element.33.basis_ref, bf16[8,2,224,128]{3,2,1,0:T(8,128)(2,1)S(1)} %all-to-all-done.2.w_ref, bf16[2,224,128]{2,1,0:T(8,128)(2,1)S(1)} %get-tuple-element.47.u0, ...), custom_call_target="tpu_custom_call" | custom-call | flops 234881024 | bytes 3145728 | tf_op jit(solution)/shard_map/back/pallas_call | solution.py:293
  110.6 5.1 %all-to-all-start.3 = ((bf16[8,224,128]{2,1,0:T(8,128)(2,1)}), bf16[8,224,128]{2,1,0:T(8,128)(2,1)}, u32[]{:S(2)}, u32[]{:S(2)}) async-start(bf16[8,224,128]{2,1,0:T(8,128)(2,1)} %back.3), calls=%async_computation.3 | async-start | bytes 917504 | tf_op jit(solution)/shard_map/all_to_all | solution.py:31
  115.7 1.8 back.2
  118.1 1.5 collective-permute-start.17
  119.6 2.1 %collective-permute-start.18 = (bf16[224,128]{1,0:T(8,128)(2,1)S(1)}, bf16[224,128]{1,0:T(8,128)(2,1)S(1)}, u32[]{:S(2)}, u32[]{:S(2)}) collective-permute-start(bf16[224,128]{1,0:T(8,128)(2,1)S(1)} %get-tuple-element.50), channel_id=1, source_target_pairs={{0,2},{1,3},{2,4},{3,5},{4,6},{5,7},{6,0},{7,1},{8,10},{9,11},{10,... | collective-permute-start | bytes 172040 | tf_op jit(solution)/shard_map/ppermute | solution.py:27
  121.7 2.4 %collective-permute-start.19 = (bf16[224,128]{1,0:T(8,128)(2,1)}, bf16[224,128]{1,0:T(8,128)(2,1)S(1)}, u32[]{:S(2)}, u32[]{:S(2)}) collective-permute-start(bf16[224,128]{1,0:T(8,128)(2,1)} %get-tuple-element.51), channel_id=1, source_target_pairs={{0,3},{1,4},{2,5},{3,6},{4,7},{5,0},{6,1},{7,2},{8,11},{9,12},{10,... | collective-permute-start | bytes 172040 | tf_op jit(solution)/shard_map/ppermute | solution.py:27
  124.1 2.5 %collective-permute-start.20 = (bf16[224,128]{1,0:T(8,128)(2,1)}, bf16[224,128]{1,0:T(8,128)(2,1)S(1)}, u32[]{:S(2)}, u32[]{:S(2)}) collective-permute-start(bf16[224,128]{1,0:T(8,128)(2,1)} %get-tuple-element.52), channel_id=1, source_target_pairs={{0,4},{1,5},{2,6},{3,7},{4,0},{5,1},{6,2},{7,3},{8,12},{9,13},{10,... | collective-permute-start | bytes 172040 | tf_op jit(solution)/shard_map/ppermute | solution.py:27
  126.6 1.9 %collective-permute-start.21 = (bf16[224,128]{1,0:T(8,128)(2,1)}, bf16[224,128]{1,0:T(8,128)(2,1)S(1)}, u32[]{:S(2)}, u32[]{:S(2)}) collective-permute-start(bf16[224,128]{1,0:T(8,128)(2,1)} %get-tuple-element.53), channel_id=1, source_target_pairs={{0,5},{1,6},{2,7},{3,0},{4,1},{5,2},{6,3},{7,4},{8,13},{9,14},{10,... | collective-permute-start | bytes 172040 | tf_op jit(solution)/shard_map/ppermute | solution.py:27
  128.6 3.3 %collective-permute-start.22 = (bf16[224,128]{1,0:T(8,128)(2,1)}, bf16[224,128]{1,0:T(8,128)(2,1)S(1)}, u32[]{:S(2)}, u32[]{:S(2)}) collective-permute-start(bf16[224,128]{1,0:T(8,128)(2,1)} %get-tuple-element.54), channel_id=1, source_target_pairs={{0,6},{1,7},{2,0},{3,1},{4,2},{5,3},{6,4},{7,5},{8,14},{9,15},{10,... | collective-permute-start | bytes 172040 | tf_op jit(solution)/shard_map/ppermute | solution.py:27
  134.3 1.3 collective-permute-start.29
  135.6 1.6 collective-permute-done.20.refs_4_
  137.1 2.5 %collective-permute-start.31 = (bf16[128,1792]{1,0:T(8,128)(2,1)S(1)}, bf16[128,1792]{1,0:T(8,128)(2,1)S(1)}, u32[]{:S(2)}, u32[]{:S(2)}) collective-permute-start(bf16[128,1792]{1,0:T(8,128)(2,1)S(1)} %bitcast.11), channel_id=1, source_target_pairs={{0,192},{64,0},{128,64},{192,128},{1,193},{65,1},{129,65},{193,129... | collective-permute-start | bytes 1376264 | tf_op jit(solution)/shard_map/ppermute | solution.py:27
  141.3 2.7 %collective-permute-start.25 = (bf16[128,1792]{1,0:T(8,128)(2,1)S(1)}, bf16[128,1792]{1,0:T(8,128)(2,1)S(1)}, u32[]{:S(2)}, u32[]{:S(2)}) collective-permute-start(bf16[128,1792]{1,0:T(8,128)(2,1)S(1)} %turn.1.refs_0_), channel_id=1, source_target_pairs={{0,192},{64,0},{128,64},{192,128},{1,193},{65,1},{129,65},{193,129... | collective-permute-start | bytes 1376264 | tf_op jit(solution)/shard_map/ppermute | solution.py:27
  144.0 5.2 %collective-permute-start.37 = (bf16[128,1792]{1,0:T(8,128)(2,1)S(1)}, bf16[128,1792]{1,0:T(8,128)(2,1)}, u32[]{:S(2)}, u32[]{:S(2)}) collective-permute-start(bf16[128,1792]{1,0:T(8,128)(2,1)S(1)} %bitcast.12), channel_id=1, source_target_pairs={{0,32},{32,0},{1,33},{33,1},{2,34},{34,2},{3,35},{35,3},{4,36},{36... | collective-permute-start | bytes 1376264 | tf_op jit(solution)/shard_map/ppermute | solution.py:27
  149.2 6.3 %collective-permute-start.35 = (bf16[128,1792]{1,0:T(8,128)(2,1)S(1)}, bf16[128,1792]{1,0:T(8,128)(2,1)}, u32[]{:S(2)}, u32[]{:S(2)}) collective-permute-start(bf16[128,1792]{1,0:T(8,128)(2,1)S(1)} %collective-permute-done.29.refs_0_), channel_id=1, source_target_pairs={{0,32},{32,0},{1,33},{33,1},{2,34},{34,2},{3,35},{35,3},{4,36},{36... | collective-permute-start | bytes 1376264 | tf_op jit(solution)/shard_map/ppermute | solution.py:27
  157.6 2.5 %collective-permute-start.32 = (bf16[64,1792]{1,0:T(8,128)(2,1)}, bf16[64,1792]{1,0:T(8,128)(2,1)}, u32[]{:S(2)}, u32[]{:S(2)}) collective-permute-start(bf16[64,1792]{1,0:T(8,128)(2,1)} %slice.17), channel_id=1, source_target_pairs={{0,192},{64,0},{128,64},{192,128},{1,193},{65,1},{129,65},{193,129... | collective-permute-start | bytes 688136 | tf_op jit(solution)/shard_map/ppermute | solution.py:27
  161.5 3.5 %all-to-all-start.4 = ((f32[8,64,224]{2,1,0:T(8,128)}), f32[8,64,224]{2,1,0:T(8,128)S(1)}, u32[]{:S(2)}, u32[]{:S(2)}) async-start(f32[8,64,224]{2,1,0:T(8,128)} %get-tuple-element.60), calls=%async_computation.4 | async-start | bytes 1048576 | tf_op jit(solution)/shard_map/all_to_all | solution.py:31
  165.0 3.9 %collective-permute-start.28 = (bf16[128,1792]{1,0:T(8,128)(2,1)S(1)}, bf16[128,1792]{1,0:T(8,128)(2,1)S(1)}, u32[]{:S(2)}, u32[]{:S(2)}) collective-permute-start(bf16[128,1792]{1,0:T(8,128)(2,1)S(1)} %turn.1.refs_0_), channel_id=1, source_target_pairs={{0,32},{32,0},{1,33},{33,1},{2,34},{34,2},{3,35},{35,3},{4,36},{36... | collective-permute-start | bytes 1376264 | tf_op jit(solution)/shard_map/ppermute | solution.py:27
  169.4 2.0 %place.6.refs_4_ = bf16[2,128,14336]{2,1,0:T(8,128)(2,1)} custom-call(s32[4]{0:T(128)S(1)} %pad_add_fusion.at_ref, bf16[128,1792]{1,0:T(8,128)(2,1)S(1)} %bitcast.13, bf16[128,1792]{1,0:T(8,128)(2,1)} %collective-permute-done.37.refs_1_), custom_call_target="tpu_custom_call" | custom-call | flops 2000000000 | bytes 1835008 | tf_op jit(solution)/shard_map/place/pallas_call | solution.py:354
  172.0 2.4 %place.7.refs_4_ = bf16[2,128,14336]{2,1,0:T(8,128)(2,1)} custom-call(s32[4]{0:T(128)S(1)} %pad_add_fusion.at_ref, bf16[128,1792]{1,0:T(8,128)(2,1)S(1)} %collective-permute-done.29.refs_0_, bf16[128,1792]{1,0:T(8,128)(2,1)S(1)} %collective-permute-done.31.refs_1_, ...), custom_call_target="tpu_custom_call", output_to_operand_aliasing={{}: (5, {})} | custom-call | flops 2000000000 | bytes 3670016 | tf_op jit(solution)/shard_map/place/pallas_call | solution.py:354
  174.6 2.6 %collective-permute-start.39 = (bf16[64,1792]{1,0:T(8,128)(2,1)S(1)}, bf16[64,1792]{1,0:T(8,128)(2,1)S(1)}, u32[]{:S(2)}, u32[]{:S(2)}) collective-permute-start(bf16[64,1792]{1,0:T(8,128)(2,1)S(1)} %copy-done.13), channel_id=1, source_target_pairs={{0,192},{64,0},{128,64},{192,128},{1,193},{65,1},{129,65},{193,129... | collective-permute-start | bytes 688136 | tf_op jit(solution)/shard_map/ppermute | solution.py:27
  177.2 1.9 %place.8.refs_2_ = bf16[2,128,14336]{2,1,0:T(8,128)(2,1)} custom-call(s32[4]{0:T(128)S(1)} %pad_add_fusion.at_ref, bf16[64,1792]{1,0:T(8,128)(2,1)S(1)} %collective-permute-done.30.refs_0_, bf16[64,1792]{1,0:T(8,128)(2,1)} %collective-permute-done.32.refs_1_, bf16[64,1792]{1,0:T(8,128)(2,1)S(1)} %collective-permute-done.33.refs_2_, ...), custom_call_target="tpu_custom_call", output_to_operand_aliasing={{}: (5, {})} | custom-call | flops 2000000000 | bytes 1835008 | tf_op jit(solution)/shard_map/place/pallas_call | solution.py:354
  179.1 1.5 place.9.refs_4_
  180.7 1.8 place.10.refs_4_
  185.3 1.5 place.11
  (100 shorter events, 25.7 us)
Async XLA Ops:
  2.8 10.4 %copy-start.6 = (bf16[2,128,1792]{2,1,0:T(8,128)(2,1)S(1)}, bf16[2,128,1792]{2,1,0:T(8,128)(2,1)}, u32[]{:S(2)}) copy-start(bf16[2,128,1792]{2,1,0:T(8,128)(2,1)} %v_ref.4) | copy-start | bytes 2752516
  4.3 20.3 %all-to-all-start.1 = ((bf16[8,144,128]{2,1,0:T(8,128)(2,1)}), bf16[8,144,128]{2,1,0:T(8,128)(2,1)S(1)}, u32[]{:S(2)}, u32[]{:S(2)}) async-start(bf16[8,144,128]{2,1,0:T(8,128)(2,1)} %pieces.1), calls=%async_computation.1 | async-start | bytes 589824 | tf_op jit(solution)/shard_map/all_to_all | solution.py:31
  24.5 28.2 %all-to-all-start = ((bf16[8,2,224,128]{3,2,1,0:T(8,128)(2,1)}), bf16[8,2,224,128]{3,2,1,0:T(8,128)(2,1)S(1)}, u32[]{:S(2)}, u32[]{:S(2)}) async-start(bf16[8,2,224,128]{3,2,1,0:T(8,128)(2,1)} %pack.2), calls=%async_computation | async-start | bytes 1835008 | tf_op jit(solution)/shard_map/all_to_all | solution.py:31
  28.1 7.6 %collective-permute-start = (bf16[8,144,128]{2,1,0:T(8,128)(2,1)S(1)}, bf16[8,144,128]{2,1,0:T(8,128)(2,1)S(1)}, u32[]{:S(2)}, u32[]{:S(2)}) collective-permute-start(bf16[8,144,128]{2,1,0:T(8,128)(2,1)S(1)} %all-to-all-done.1), channel_id=1, source_target_pairs={{0,64},{64,128},{128,192},{192,0},{1,65},{65,129},{129,193},{193,1... | collective-permute-start | bytes 884744 | tf_op jit(solution)/shard_map/ppermute | solution.py:27
  29.4 13.6 %collective-permute-start.1 = (bf16[8,144,128]{2,1,0:T(8,128)(2,1)S(1)}, bf16[8,144,128]{2,1,0:T(8,128)(2,1)S(1)}, u32[]{:S(2)}, u32[]{:S(2)}) collective-permute-start(bf16[8,144,128]{2,1,0:T(8,128)(2,1)S(1)} %all-to-all-done.1), channel_id=1, source_target_pairs={{0,128},{64,192},{128,0},{192,64},{1,129},{65,193},{129,1},{193,65... | collective-permute-start | bytes 884744 | tf_op jit(solution)/shard_map/ppermute | solution.py:27
  31.8 11.5 %collective-permute-start.2 = (bf16[8,144,128]{2,1,0:T(8,128)(2,1)S(1)}, bf16[8,144,128]{2,1,0:T(8,128)(2,1)S(1)}, u32[]{:S(2)}, u32[]{:S(2)}) collective-permute-start(bf16[8,144,128]{2,1,0:T(8,128)(2,1)S(1)} %all-to-all-done.1), channel_id=1, source_target_pairs={{0,192},{64,0},{128,64},{192,128},{1,193},{65,1},{129,65},{193,129... | collective-permute-start | bytes 884744 | tf_op jit(solution)/shard_map/ppermute | solution.py:27
  43.5 12.8 %collective-permute-start.3 = (bf16[4,8,144,128]{3,2,1,0:T(8,128)(2,1)S(1)}, bf16[4,8,144,128]{3,2,1,0:T(8,128)(2,1)}, u32[]{:S(2)}, u32[]{:S(2)}) collective-permute-start(bf16[4,8,144,128]{3,2,1,0:T(8,128)(2,1)S(1)} %pad_maximum_fusion.own_ref), channel_id=1, source_target_pairs={{0,32},{32,0},{1,33},{33,1},{2,34},{34,2},{3,35},{35,3},{4,36},{36... | collective-permute-start | bytes 3538952 | tf_op jit(solution)/shard_map/ppermute | solution.py:27
  52.8 54.7 %all-to-all-start.2 = ((bf16[8,2,224,128]{3,2,1,0:T(8,128)(2,1)}), bf16[8,2,224,128]{3,2,1,0:T(8,128)(2,1)S(1)}, u32[]{:S(2)}, u32[]{:S(2)}) async-start(bf16[8,2,224,128]{3,2,1,0:T(8,128)(2,1)} %copy-done.4), calls=%async_computation.2 | async-start | bytes 1835008 | tf_op jit(solution)/shard_map/all_to_all | solution.py:31
  61.6 25.2 %collective-permute-start.4 = (f32[2,232,128]{2,1,0:T(8,128)S(1)}, f32[2,232,128]{2,1,0:T(8,128)S(1)}, u32[]{:S(2)}, u32[]{:S(2)}) collective-permute-start(f32[2,232,128]{2,1,0:T(8,128)S(1)} %get-tuple-element.36), channel_id=1, source_target_pairs={{0,8},{8,16},{16,24},{24,0},{1,9},{9,17},{17,25},{25,1},{2,10},{10... | collective-permute-start | bytes 712712 | tf_op jit(solution)/shard_map/ppermute | solution.py:27
  62.9 26.7 %collective-permute-start.5 = (f32[2,232,128]{2,1,0:T(8,128)S(1)}, f32[2,232,128]{2,1,0:T(8,128)S(1)}, u32[]{:S(2)}, u32[]{:S(2)}) collective-permute-start(f32[2,232,128]{2,1,0:T(8,128)S(1)} %get-tuple-element.37), channel_id=1, source_target_pairs={{0,16},{8,24},{16,0},{24,8},{1,17},{9,25},{17,1},{25,9},{2,18},{10... | collective-permute-start | bytes 712712 | tf_op jit(solution)/shard_map/ppermute | solution.py:27
  65.5 25.3 %collective-permute-start.6 = (f32[2,232,128]{2,1,0:T(8,128)S(1)}, f32[2,232,128]{2,1,0:T(8,128)S(1)}, u32[]{:S(2)}, u32[]{:S(2)}) collective-permute-start(f32[2,232,128]{2,1,0:T(8,128)S(1)} %get-tuple-element.38), channel_id=1, source_target_pairs={{0,24},{8,0},{16,8},{24,16},{1,25},{9,1},{17,9},{25,17},{2,26},{10... | collective-permute-start | bytes 712712 | tf_op jit(solution)/shard_map/ppermute | solution.py:27
  67.4 16.8 %collective-permute-start.10 = (f32[64,224]{1,0:T(8,128)S(1)}, f32[64,224]{1,0:T(8,128)S(1)}, u32[]{:S(2)}, u32[]{:S(2)}) collective-permute-start(f32[64,224]{1,0:T(8,128)S(1)} %get-tuple-element.43), channel_id=1, source_target_pairs={{0,4},{1,5},{2,6},{3,7},{4,0},{5,1},{6,2},{7,3},{8,12},{9,13},{10,... | collective-permute-start | bytes 172040 | tf_op jit(solution)/shard_map/ppermute | solution.py:27
  72.8 11.5 %collective-permute-start.11 = (f32[64,224]{1,0:T(8,128)S(1)}, f32[64,224]{1,0:T(8,128)S(1)}, u32[]{:S(2)}, u32[]{:S(2)}) collective-permute-start(f32[64,224]{1,0:T(8,128)S(1)} %get-tuple-element.44), channel_id=1, source_target_pairs={{0,5},{1,6},{2,7},{3,0},{4,1},{5,2},{6,3},{7,4},{8,13},{9,14},{10,... | collective-permute-start | bytes 172040 | tf_op jit(solution)/shard_map/ppermute | solution.py:27
  84.2 6.7 %collective-permute-start.12 = (f32[64,224]{1,0:T(8,128)S(1)}, f32[64,224]{1,0:T(8,128)S(1)}, u32[]{:S(2)}, u32[]{:S(2)}) collective-permute-start(f32[64,224]{1,0:T(8,128)S(1)} %get-tuple-element.45), channel_id=1, source_target_pairs={{0,6},{1,7},{2,0},{3,1},{4,2},{5,3},{6,4},{7,5},{8,14},{9,15},{10,... | collective-permute-start | bytes 172040 | tf_op jit(solution)/shard_map/ppermute | solution.py:27
  84.2 7.3 %collective-permute-start.13 = (f32[64,224]{1,0:T(8,128)S(1)}, f32[64,224]{1,0:T(8,128)S(1)}, u32[]{:S(2)}, u32[]{:S(2)}) collective-permute-start(f32[64,224]{1,0:T(8,128)S(1)} %get-tuple-element.46), channel_id=1, source_target_pairs={{0,7},{1,0},{2,1},{3,2},{4,3},{5,4},{6,5},{7,6},{8,15},{9,8},{10,9... | collective-permute-start | bytes 172040 | tf_op jit(solution)/shard_map/ppermute | solution.py:27
  86.8 4.7 %collective-permute-start.7 = (f32[64,224]{1,0:T(8,128)S(1)}, f32[64,224]{1,0:T(8,128)S(1)}, u32[]{:S(2)}, u32[]{:S(2)}) collective-permute-start(f32[64,224]{1,0:T(8,128)S(1)} %get-tuple-element.40), channel_id=1, source_target_pairs={{0,1},{1,2},{2,3},{3,4},{4,5},{5,6},{6,7},{7,0},{8,9},{9,10},{10,1... | collective-permute-start | bytes 172040 | tf_op jit(solution)/shard_map/ppermute | solution.py:27
  89.6 5.7 %collective-permute-start.8 = (f32[64,224]{1,0:T(8,128)S(1)}, f32[64,224]{1,0:T(8,128)S(1)}, u32[]{:S(2)}, u32[]{:S(2)}) collective-permute-start(f32[64,224]{1,0:T(8,128)S(1)} %get-tuple-element.41), channel_id=1, source_target_pairs={{0,2},{1,3},{2,4},{3,5},{4,6},{5,7},{6,0},{7,1},{8,10},{9,11},{10,... | collective-permute-start | bytes 172040 | tf_op jit(solution)/shard_map/ppermute | solution.py:27
  90.9 8.3 %collective-permute-start.9 = (f32[64,224]{1,0:T(8,128)S(1)}, f32[64,224]{1,0:T(8,128)S(1)}, u32[]{:S(2)}, u32[]{:S(2)}) collective-permute-start(f32[64,224]{1,0:T(8,128)S(1)} %get-tuple-element.42), channel_id=1, source_target_pairs={{0,3},{1,4},{2,5},{3,6},{4,7},{5,0},{6,1},{7,2},{8,11},{9,12},{10,... | collective-permute-start | bytes 172040 | tf_op jit(solution)/shard_map/ppermute | solution.py:27
  100.8 6.1 %collective-permute-start.14 = (bf16[2,224,128]{2,1,0:T(8,128)(2,1)S(1)}, bf16[2,224,128]{2,1,0:T(8,128)(2,1)S(1)}, u32[]{:S(2)}, u32[]{:S(2)}) collective-permute-start(bf16[2,224,128]{2,1,0:T(8,128)(2,1)S(1)} %get-tuple-element.47.u0), channel_id=1, source_target_pairs={{0,8},{8,16},{16,24},{24,0},{1,9},{9,17},{17,25},{25,1},{2,10},{10... | collective-permute-start | bytes 344072 | tf_op jit(solution)/shard_map/ppermute | solution.py:27
  100.8 6.1 %collective-permute-start.15 = (bf16[2,224,128]{2,1,0:T(8,128)(2,1)S(1)}, bf16[2,224,128]{2,1,0:T(8,128)(2,1)S(1)}, u32[]{:S(2)}, u32[]{:S(2)}) collective-permute-start(bf16[2,224,128]{2,1,0:T(8,128)(2,1)S(1)} %get-tuple-element.47.u0), channel_id=1, source_target_pairs={{0,16},{8,24},{16,0},{24,8},{1,17},{9,25},{17,1},{25,9},{2,18},{10... | collective-permute-start | bytes 344072 | tf_op jit(solution)/shard_map/ppermute | solution.py:27
  100.8 6.7 %collective-permute-start.16 = (bf16[2,224,128]{2,1,0:T(8,128)(2,1)S(1)}, bf16[2,224,128]{2,1,0:T(8,128)(2,1)S(1)}, u32[]{:S(2)}, u32[]{:S(2)}) collective-permute-start(bf16[2,224,128]{2,1,0:T(8,128)(2,1)S(1)} %get-tuple-element.47.u0), channel_id=1, source_target_pairs={{0,24},{8,0},{16,8},{24,16},{1,25},{9,1},{17,9},{25,17},{2,26},{10... | collective-permute-start | bytes 344072 | tf_op jit(solution)/shard_map/ppermute | solution.py:27
  110.6 22.4 %all-to-all-start.3 = ((bf16[8,224,128]{2,1,0:T(8,128)(2,1)}), bf16[8,224,128]{2,1,0:T(8,128)(2,1)}, u32[]{:S(2)}, u32[]{:S(2)}) async-start(bf16[8,224,128]{2,1,0:T(8,128)(2,1)} %back.3), calls=%async_computation.3 | async-start | bytes 917504 | tf_op jit(solution)/shard_map/all_to_all | solution.py:31
  118.1 10.4 %collective-permute-start.17 = (bf16[224,128]{1,0:T(8,128)(2,1)S(1)}, bf16[224,128]{1,0:T(8,128)(2,1)S(1)}, u32[]{:S(2)}, u32[]{:S(2)}) collective-permute-start(bf16[224,128]{1,0:T(8,128)(2,1)S(1)} %get-tuple-element.49), channel_id=1, source_target_pairs={{0,1},{1,2},{2,3},{3,4},{4,5},{5,6},{6,7},{7,0},{8,9},{9,10},{10,1... | collective-permute-start | bytes 172040 | tf_op jit(solution)/shard_map/ppermute | solution.py:27
  119.6 12.3 %collective-permute-start.18 = (bf16[224,128]{1,0:T(8,128)(2,1)S(1)}, bf16[224,128]{1,0:T(8,128)(2,1)S(1)}, u32[]{:S(2)}, u32[]{:S(2)}) collective-permute-start(bf16[224,128]{1,0:T(8,128)(2,1)S(1)} %get-tuple-element.50), channel_id=1, source_target_pairs={{0,2},{1,3},{2,4},{3,5},{4,6},{5,7},{6,0},{7,1},{8,10},{9,11},{10,... | collective-permute-start | bytes 172040 | tf_op jit(solution)/shard_map/ppermute | solution.py:27
  121.7 12.6 %collective-permute-start.19 = (bf16[224,128]{1,0:T(8,128)(2,1)}, bf16[224,128]{1,0:T(8,128)(2,1)S(1)}, u32[]{:S(2)}, u32[]{:S(2)}) collective-permute-start(bf16[224,128]{1,0:T(8,128)(2,1)} %get-tuple-element.51), channel_id=1, source_target_pairs={{0,3},{1,4},{2,5},{3,6},{4,7},{5,0},{6,1},{7,2},{8,11},{9,12},{10,... | collective-permute-start | bytes 172040 | tf_op jit(solution)/shard_map/ppermute | solution.py:27
  124.1 13.1 %collective-permute-start.20 = (bf16[224,128]{1,0:T(8,128)(2,1)}, bf16[224,128]{1,0:T(8,128)(2,1)S(1)}, u32[]{:S(2)}, u32[]{:S(2)}) collective-permute-start(bf16[224,128]{1,0:T(8,128)(2,1)} %get-tuple-element.52), channel_id=1, source_target_pairs={{0,4},{1,5},{2,6},{3,7},{4,0},{5,1},{6,2},{7,3},{8,12},{9,13},{10,... | collective-permute-start | bytes 172040 | tf_op jit(solution)/shard_map/ppermute | solution.py:27
  126.6 13.0 %collective-permute-start.21 = (bf16[224,128]{1,0:T(8,128)(2,1)}, bf16[224,128]{1,0:T(8,128)(2,1)S(1)}, u32[]{:S(2)}, u32[]{:S(2)}) collective-permute-start(bf16[224,128]{1,0:T(8,128)(2,1)} %get-tuple-element.53), channel_id=1, source_target_pairs={{0,5},{1,6},{2,7},{3,0},{4,1},{5,2},{6,3},{7,4},{8,13},{9,14},{10,... | collective-permute-start | bytes 172040 | tf_op jit(solution)/shard_map/ppermute | solution.py:27
  128.6 11.1 %collective-permute-start.22 = (bf16[224,128]{1,0:T(8,128)(2,1)}, bf16[224,128]{1,0:T(8,128)(2,1)S(1)}, u32[]{:S(2)}, u32[]{:S(2)}) collective-permute-start(bf16[224,128]{1,0:T(8,128)(2,1)} %get-tuple-element.54), channel_id=1, source_target_pairs={{0,6},{1,7},{2,0},{3,1},{4,2},{5,3},{6,4},{7,5},{8,14},{9,15},{10,... | collective-permute-start | bytes 172040 | tf_op jit(solution)/shard_map/ppermute | solution.py:27
  131.8 7.8 %collective-permute-start.23 = (bf16[224,128]{1,0:T(8,128)(2,1)}, bf16[224,128]{1,0:T(8,128)(2,1)S(1)}, u32[]{:S(2)}, u32[]{:S(2)}) collective-permute-start(bf16[224,128]{1,0:T(8,128)(2,1)} %get-tuple-element.55), channel_id=1, source_target_pairs={{0,7},{1,0},{2,1},{3,2},{4,3},{5,4},{6,5},{7,6},{8,15},{9,8},{10,9... | collective-permute-start | bytes 172040 | tf_op jit(solution)/shard_map/ppermute | solution.py:27
  134.3 14.9 %collective-permute-start.29 = (bf16[128,1792]{1,0:T(8,128)(2,1)S(1)}, bf16[128,1792]{1,0:T(8,128)(2,1)S(1)}, u32[]{:S(2)}, u32[]{:S(2)}) collective-permute-start(bf16[128,1792]{1,0:T(8,128)(2,1)S(1)} %bitcast.10), channel_id=1, source_target_pairs={{0,64},{64,128},{128,192},{192,0},{1,65},{65,129},{129,193},{193,1... | collective-permute-start | bytes 1376264 | tf_op jit(solution)/shard_map/ppermute | solution.py:27
  137.1 18.3 %collective-permute-start.31 = (bf16[128,1792]{1,0:T(8,128)(2,1)S(1)}, bf16[128,1792]{1,0:T(8,128)(2,1)S(1)}, u32[]{:S(2)}, u32[]{:S(2)}) collective-permute-start(bf16[128,1792]{1,0:T(8,128)(2,1)S(1)} %bitcast.11), channel_id=1, source_target_pairs={{0,192},{64,0},{128,64},{192,128},{1,193},{65,1},{129,65},{193,129... | collective-permute-start | bytes 1376264 | tf_op jit(solution)/shard_map/ppermute | solution.py:27
  141.2 15.6 %collective-permute-start.24 = (bf16[128,1792]{1,0:T(8,128)(2,1)S(1)}, bf16[128,1792]{1,0:T(8,128)(2,1)S(1)}, u32[]{:S(2)}, u32[]{:S(2)}) collective-permute-start(bf16[128,1792]{1,0:T(8,128)(2,1)S(1)} %turn.1.refs_0_), channel_id=1, source_target_pairs={{0,64},{64,128},{128,192},{192,0},{1,65},{65,129},{129,193},{193,1... | collective-permute-start | bytes 1376264 | tf_op jit(solution)/shard_map/ppermute | solution.py:27
  141.3 16.3 %collective-permute-start.25 = (bf16[128,1792]{1,0:T(8,128)(2,1)S(1)}, bf16[128,1792]{1,0:T(8,128)(2,1)S(1)}, u32[]{:S(2)}, u32[]{:S(2)}) collective-permute-start(bf16[128,1792]{1,0:T(8,128)(2,1)S(1)} %turn.1.refs_0_), channel_id=1, source_target_pairs={{0,192},{64,0},{128,64},{192,128},{1,193},{65,1},{129,65},{193,129... | collective-permute-start | bytes 1376264 | tf_op jit(solution)/shard_map/ppermute | solution.py:27
  144.0 21.0 %collective-permute-start.37 = (bf16[128,1792]{1,0:T(8,128)(2,1)S(1)}, bf16[128,1792]{1,0:T(8,128)(2,1)}, u32[]{:S(2)}, u32[]{:S(2)}) collective-permute-start(bf16[128,1792]{1,0:T(8,128)(2,1)S(1)} %bitcast.12), channel_id=1, source_target_pairs={{0,32},{32,0},{1,33},{33,1},{2,34},{34,2},{3,35},{35,3},{4,36},{36... | collective-permute-start | bytes 1376264 | tf_op jit(solution)/shard_map/ppermute | solution.py:27
  149.2 22.2 %collective-permute-start.35 = (bf16[128,1792]{1,0:T(8,128)(2,1)S(1)}, bf16[128,1792]{1,0:T(8,128)(2,1)}, u32[]{:S(2)}, u32[]{:S(2)}) collective-permute-start(bf16[128,1792]{1,0:T(8,128)(2,1)S(1)} %collective-permute-done.29.refs_0_), channel_id=1, source_target_pairs={{0,32},{32,0},{1,33},{33,1},{2,34},{34,2},{3,35},{35,3},{4,36},{36... | collective-permute-start | bytes 1376264 | tf_op jit(solution)/shard_map/ppermute | solution.py:27
  155.4 16.2 %collective-permute-start.36 = (bf16[128,1792]{1,0:T(8,128)(2,1)S(1)}, bf16[128,1792]{1,0:T(8,128)(2,1)}, u32[]{:S(2)}, u32[]{:S(2)}) collective-permute-start(bf16[128,1792]{1,0:T(8,128)(2,1)S(1)} %collective-permute-done.31.refs_1_), channel_id=1, source_target_pairs={{0,32},{32,0},{1,33},{33,1},{2,34},{34,2},{3,35},{35,3},{4,36},{36... | collective-permute-start | bytes 1376264 | tf_op jit(solution)/shard_map/ppermute | solution.py:27
  156.8 12.0 %collective-permute-start.30 = (bf16[64,1792]{1,0:T(8,128)(2,1)}, bf16[64,1792]{1,0:T(8,128)(2,1)S(1)}, u32[]{:S(2)}, u32[]{:S(2)}) collective-permute-start(bf16[64,1792]{1,0:T(8,128)(2,1)} %slice.16), channel_id=1, source_target_pairs={{0,64},{64,128},{128,192},{192,0},{1,65},{65,129},{129,193},{193,1... | collective-permute-start | bytes 688136 | tf_op jit(solution)/shard_map/ppermute | solution.py:27
  157.6 11.4 %collective-permute-start.32 = (bf16[64,1792]{1,0:T(8,128)(2,1)}, bf16[64,1792]{1,0:T(8,128)(2,1)}, u32[]{:S(2)}, u32[]{:S(2)}) collective-permute-start(bf16[64,1792]{1,0:T(8,128)(2,1)} %slice.17), channel_id=1, source_target_pairs={{0,192},{64,0},{128,64},{192,128},{1,193},{65,1},{129,65},{193,129... | collective-permute-start | bytes 688136 | tf_op jit(solution)/shard_map/ppermute | solution.py:27
  161.5 22.3 %all-to-all-start.4 = ((f32[8,64,224]{2,1,0:T(8,128)}), f32[8,64,224]{2,1,0:T(8,128)S(1)}, u32[]{:S(2)}, u32[]{:S(2)}) async-start(f32[8,64,224]{2,1,0:T(8,128)} %get-tuple-element.60), calls=%async_computation.4 | async-start | bytes 1048576 | tf_op jit(solution)/shard_map/all_to_all | solution.py:31
  165.0 14.1 %collective-permute-start.28 = (bf16[128,1792]{1,0:T(8,128)(2,1)S(1)}, bf16[128,1792]{1,0:T(8,128)(2,1)S(1)}, u32[]{:S(2)}, u32[]{:S(2)}) collective-permute-start(bf16[128,1792]{1,0:T(8,128)(2,1)S(1)} %turn.1.refs_0_), channel_id=1, source_target_pairs={{0,32},{32,0},{1,33},{33,1},{2,34},{34,2},{3,35},{35,3},{4,36},{36... | collective-permute-start | bytes 1376264 | tf_op jit(solution)/shard_map/ppermute | solution.py:27
  168.9 5.6 %collective-permute-start.33 = (bf16[64,1792]{1,0:T(8,128)(2,1)S(1)}, bf16[64,1792]{1,0:T(8,128)(2,1)S(1)}, u32[]{:S(2)}, u32[]{:S(2)}) collective-permute-start(bf16[64,1792]{1,0:T(8,128)(2,1)S(1)} %collective-permute-done.30.refs_0_), channel_id=1, source_target_pairs={{0,32},{32,0},{1,33},{33,1},{2,34},{34,2},{3,35},{35,3},{4,36},{36... | collective-permute-start | bytes 688136 | tf_op jit(solution)/shard_map/ppermute | solution.py:27
  169.0 5.6 %collective-permute-start.34 = (bf16[64,1792]{1,0:T(8,128)(2,1)}, bf16[64,1792]{1,0:T(8,128)(2,1)S(1)}, u32[]{:S(2)}, u32[]{:S(2)}) collective-permute-start(bf16[64,1792]{1,0:T(8,128)(2,1)} %collective-permute-done.32.refs_1_), channel_id=1, source_target_pairs={{0,32},{32,0},{1,33},{33,1},{2,34},{34,2},{3,35},{35,3},{4,36},{36... | collective-permute-start | bytes 688136 | tf_op jit(solution)/shard_map/ppermute | solution.py:27
  171.4 9.2 %collective-permute-start.26 = (bf16[128,1792]{1,0:T(8,128)(2,1)S(1)}, bf16[128,1792]{1,0:T(8,128)(2,1)S(1)}, u32[]{:S(2)}, u32[]{:S(2)}) collective-permute-start(bf16[128,1792]{1,0:T(8,128)(2,1)S(1)} %collective-permute-done.24.refs_0_), channel_id=1, source_target_pairs={{0,32},{32,0},{1,33},{33,1},{2,34},{34,2},{3,35},{35,3},{4,36},{36... | collective-permute-start | bytes 1376264 | tf_op jit(solution)/shard_map/ppermute | solution.py:27
  171.6 9.1 %collective-permute-start.27 = (bf16[128,1792]{1,0:T(8,128)(2,1)S(1)}, bf16[128,1792]{1,0:T(8,128)(2,1)S(1)}, u32[]{:S(2)}, u32[]{:S(2)}) collective-permute-start(bf16[128,1792]{1,0:T(8,128)(2,1)S(1)} %collective-permute-done.25.refs_1_), channel_id=1, source_target_pairs={{0,32},{32,0},{1,33},{33,1},{2,34},{34,2},{3,35},{35,3},{4,36},{36... | collective-permute-start | bytes 1376264 | tf_op jit(solution)/shard_map/ppermute | solution.py:27
  174.5 8.3 %collective-permute-start.38 = (bf16[64,1792]{1,0:T(8,128)(2,1)S(1)}, bf16[64,1792]{1,0:T(8,128)(2,1)S(1)}, u32[]{:S(2)}, u32[]{:S(2)}) collective-permute-start(bf16[64,1792]{1,0:T(8,128)(2,1)S(1)} %copy-done.14), channel_id=1, source_target_pairs={{0,64},{64,128},{128,192},{192,0},{1,65},{65,129},{129,193},{193,1... | collective-permute-start | bytes 688136 | tf_op jit(solution)/shard_map/ppermute | solution.py:27
  174.6 8.2 %collective-permute-start.39 = (bf16[64,1792]{1,0:T(8,128)(2,1)S(1)}, bf16[64,1792]{1,0:T(8,128)(2,1)S(1)}, u32[]{:S(2)}, u32[]{:S(2)}) collective-permute-start(bf16[64,1792]{1,0:T(8,128)(2,1)S(1)} %copy-done.13), channel_id=1, source_target_pairs={{0,192},{64,0},{128,64},{192,128},{1,193},{65,1},{129,65},{193,129... | collective-permute-start | bytes 688136 | tf_op jit(solution)/shard_map/ppermute | solution.py:27
  182.8 2.1 %collective-permute-start.40 = (bf16[64,1792]{1,0:T(8,128)(2,1)S(1)}, bf16[64,1792]{1,0:T(8,128)(2,1)S(1)}, u32[]{:S(2)}, u32[]{:S(2)}) collective-permute-start(bf16[64,1792]{1,0:T(8,128)(2,1)S(1)} %collective-permute-done.38.refs_0_), channel_id=1, source_target_pairs={{0,32},{32,0},{1,33},{33,1},{2,34},{34,2},{3,35},{35,3},{4,36},{36... | collective-permute-start | bytes 688136 | tf_op jit(solution)/shard_map/ppermute | solution.py:27
  183.8 1.5 collective-permute-start.41
  (14 other events, 38.6 us)

commit v2 on v1

--- a/solution.py
+++ b/solution.py
@@ -325,12 +325,12 @@
     )(at, *blocks)
 
 
-def place_kernel(m, spots, at_ref, *refs):
+def place_kernel(spots, at_ref, *refs):
     n = len(spots)
     blocks, out_ref, sems = refs[:n], refs[-2], refs[-1]
     x, core = at_ref[0], at_ref[1]
     copies = []
-    for i, (dx, across, row) in enumerate(spots):
+    for i, (m, dx, across, row) in enumerate(spots):
         rows, width = blocks[i].shape
         owner = lax.rem(x + dx, 4) * 2 + (1 - core if across else core)
         start = pl.multiple_of(owner * width, 128)
@@ -345,14 +345,14 @@
         copy.wait()
 
 
-def place(whole, shape, m, at, items):
+def place(whole, shape, at, items):
     spots = [item[1:] for item in items]
     blocks = [item[0] for item in items]
     n = len(blocks)
     given = () if whole is None else (whole,)
     size = sum(2 * 2 * b.size for b in blocks)
     return pl.pallas_call(
-        functools.partial(place_kernel, m, spots),
+        functools.partial(place_kernel, spots),
         out_shape=jax.ShapeDtypeStruct(shape, BF16),
         in_specs=[SMEM] + [VMEM] * n + [ANY] * len(given),
         out_specs=ANY,
@@ -401,32 +401,35 @@
     half = rows // 2
     shape = (mats, rows, cols * nx * nc)
 
-    def put(whole, m, items):
-        there = [(shift(b, "core", 1), dx, True, row) for b, dx, row in items]
-        here = [(b, dx, False, row) for b, dx, row in items]
-        return place(whole, shape, m, at, here + there)
+    def both(m, items):
+        there = [(shift(b, "core", 1), m, dx, True, row) for b, dx, row in items]
+        return [(b, m, dx, False, row) for b, dx, row in items] + there
+
+    def put(whole, items):
+        return place(whole, shape, at, items)
 
     near = []
     for f in fresh:
-        near.append((shift(f, "x", 1), shift(f, "x", -1)))
+        left = shift(f, "x", 1)
+        right = shift(f, "x", -1)
+        near.append((left, right))
 
     def far(left, right):
         return shift(left[:half], "x", 1), shift(right[half:], "x", -1)
 
-    def put_near(whole, m):
-        whole = put(whole, m, [(fresh[m], 0, 0)])
-        return put(whole, m, [(near[m][0], 3, 0), (near[m][1], 1, 0)])
-
-    def put_far(whole, m, top, low):
-        return put(whole, m, [(top, 2, 0), (low, 2, half)])
+    def close(m):
+        items = [(fresh[m], 0, 0), (near[m][0], 3, 0), (near[m][1], 1, 0)]
+        return both(m, items)
+
+    def distant(m, top, low):
+        return both(m, [(top, 2, 0), (low, 2, half)])
 
     first = far(*near[0])
-    whole = put_near(None, 0)
+    whole = put(None, close(0))
     second = far(*near[1])
-    whole = put_far(whole, 0, *first)
-    whole = put_near(whole, 1)
+    whole = put(whole, distant(0, *first) + close(1))
     whole, *second = lax.optimization_barrier((whole, *second))
-    whole = put_far(whole, 1, *second)
+    whole = put(whole, distant(1, *second))
     return (whole, news[0], news[1])
 
 

time: 188 us -> 200 us (1.064)
  waiting for transfers between devices: 51.6 us -> 78.3 us
  starting transfers between devices: 97.2 us -> 89.2 us
  Pallas kernels: 25.8 us -> 21.8 us
  local copies, waits for them, and re-layouts: 11 us -> 8.27 us
    ppermute x42, waiting for transfers between devices: 36.4 us -> 65.6 us  [shift(): return lax.ppermute(v, axis, [(i, (i + k) % n) for i in range(n)])]
    ppermute x42, starting transfers between devices: 72.5 us -> 63.7 us  [shift(): return lax.ppermute(v, axis, [(i, (i + k) % n) for i in range(n)])]
    pallas_call x6 -> x3, Pallas kernels: 11.1 us -> 7.74 us  [place(): pl.pallas_call(functools.partial(place_kernel, spots), out_shape=jax.Shap...]
    slice x4, local copies, waits for them, and re-layouts: 2.81 us -> 0.07 us  [far(): return (shift(left[:half], 'x', 1), shift(right[half:], 'x', -1))]
    all_to_all x5, waiting for transfers between devices: 15.2 us -> 12.7 us  [exchange(): return lax.all_to_all(v, axis, split_axis=0, concat_axis=0, tiled=True)]
    unnamed x30 -> x26, local copies, waits for them, and re-layouts: 6.96 us -> 6.98 us
  transfers between devices with their start and end apart: 47 -> 47, of which waited for: 15 -> 23; matrix products, arithmetic and copies ran while one was open for 2% -> 1% of each run, Pallas kernels for 11% -> 8%
where the time goes in v2:
time: 200 us; the launch traced here: 199 us
  starting transfers between devices  89.2 us (45%)
  waiting for transfers between devices  78.3 us (39%)
  Pallas kernels  21.8 us (11%)
  local copies, waits for them, and re-layouts  8.27 us (4%)
    ppermute x42, waiting for transfers between devices, shift(): return lax.ppermute(v, axis, [(i, (i + k) % n) for i in range(n)])  65.6 us
    ppermute x42, starting transfers between devices, shift(): return lax.ppermute(v, axis, [(i, (i + k) % n) for i in range(n)])  63.7 us
    all_to_all x5, starting transfers between devices, exchange(): return lax.all_to_all(v, axis, split_axis=0, concat_axis=0, tiled=True)  25.5 us
    all_to_all x5, waiting for transfers between devices, exchange(): return lax.all_to_all(v, axis, split_axis=0, concat_axis=0, tiled=True)  12.7 us
    pallas_call x3, Pallas kernels, place(): pl.pallas_call(functools.partial(place_kernel, spots), out_shape=jax.Shap...  7.74 us
    unnamed x26, local copies, waits for them, and re-layouts  6.98 us
    pallas_call x2, Pallas kernels, back(): pl.pallas_call(functools.partial(back_kernel, m), out_shape=[jax.ShapeDty...  4.37 us
  transfers between devices with their start and end apart: 47, of which 23 were waited for; matrix products, arithmetic and copies ran while one was open for 1% of the time, Pallas kernels for 8%

profile of v2, /device:TPU:1, one launch (start us, length us, event | category | flops | bytes accessed | tf_op | source)
XLA Modules:
  0.0 198.9 jit_solution(12896717726949841001)
XLA Ops:
  4.3 9.0 %all-to-all-start.1 = ((bf16[8,144,128]{2,1,0:T(8,128)(2,1)}), bf16[8,144,128]{2,1,0:T(8,128)(2,1)S(1)}, u32[]{:S(2)}, u32[]{:S(2)}) async-start(bf16[8,144,128]{2,1,0:T(8,128)(2,1)} %pieces.1), calls=%async_computation.1 | async-start | bytes 589824 | tf_op jit(solution)/shard_map/all_to_all | solution.py:31
  14.5 10.0 %all-to-all-done.1 = bf16[8,144,128]{2,1,0:T(8,128)(2,1)S(1)} async-done(((bf16[8,144,128]{2,1,0:T(8,128)(2,1)}), bf16[8,144,128]{2,1,0:T(8,128)(2,1)S(1)}, u32[]{:S(2)}, u32[]{:S(2)}) %all-to-all-start.1) | async-done | bytes 294944 | tf_op jit(solution)/shard_map/all_to_all | solution.py:31
  24.5 3.6 %all-to-all-start = ((bf16[8,2,224,128]{3,2,1,0:T(8,128)(2,1)}), bf16[8,2,224,128]{3,2,1,0:T(8,128)(2,1)S(1)}, u32[]{:S(2)}, u32[]{:S(2)}) async-start(bf16[8,2,224,128]{3,2,1,0:T(8,128)(2,1)} %pack.2), calls=%async_computation | async-start | bytes 1835008 | tf_op jit(solution)/shard_map/all_to_all | solution.py:31
  28.1 2.6 %collective-permute-start.2 = (bf16[8,144,128]{2,1,0:T(8,128)(2,1)S(1)}, bf16[8,144,128]{2,1,0:T(8,128)(2,1)S(1)}, u32[]{:S(2)}, u32[]{:S(2)}) collective-permute-start(bf16[8,144,128]{2,1,0:T(8,128)(2,1)S(1)} %all-to-all-done.1), channel_id=1, source_target_pairs={{0,192},{64,0},{128,64},{192,128},{1,193},{65,1},{129,65},{193,129... | collective-permute-start | bytes 884744 | tf_op jit(solution)/shard_map/ppermute | solution.py:27
  31.8 4.2 %collective-permute-done.2 = bf16[8,144,128]{2,1,0:T(8,128)(2,1)S(1)} collective-permute-done((bf16[8,144,128]{2,1,0:T(8,128)(2,1)S(1)}, bf16[8,144,128]{2,1,0:T(8,128)(2,1)S(1)}, u32[]{:S(2)}, u32[]{:S(2)}) %collective-permute-start.2) | collective-permute-done | bytes 294944 | tf_op jit(solution)/shard_map/ppermute | solution.py:27
  36.0 2.3 %collective-permute-done.1 = bf16[8,144,128]{2,1,0:T(8,128)(2,1)S(1)} collective-permute-done((bf16[8,144,128]{2,1,0:T(8,128)(2,1)S(1)}, bf16[8,144,128]{2,1,0:T(8,128)(2,1)S(1)}, u32[]{:S(2)}, u32[]{:S(2)}) %collective-permute-start.1) | collective-permute-done | bytes 294944 | tf_op jit(solution)/shard_map/ppermute | solution.py:27
  38.2 9.1 %collective-permute-done = bf16[8,144,128]{2,1,0:T(8,128)(2,1)S(1)} collective-permute-done((bf16[8,144,128]{2,1,0:T(8,128)(2,1)S(1)}, bf16[8,144,128]{2,1,0:T(8,128)(2,1)S(1)}, u32[]{:S(2)}, u32[]{:S(2)}) %collective-permute-start) | collective-permute-done | bytes 294944 | tf_op jit(solution)/shard_map/ppermute | solution.py:27
  50.1 2.7 %all-to-all-done.g_ref = bf16[8,2,224,128]{3,2,1,0:T(8,128)(2,1)S(1)} async-done(((bf16[8,2,224,128]{3,2,1,0:T(8,128)(2,1)}), bf16[8,2,224,128]{3,2,1,0:T(8,128)(2,1)S(1)}, u32[]{:S(2)}, u32[]{:S(2)}) %all-to-all-start) | async-done | bytes 917536 | tf_op jit(solution)/shard_map/all_to_all | solution.py:31
  52.8 3.6 %all-to-all-start.2 = ((bf16[8,2,224,128]{3,2,1,0:T(8,128)(2,1)}), bf16[8,2,224,128]{3,2,1,0:T(8,128)(2,1)S(1)}, u32[]{:S(2)}, u32[]{:S(2)}) async-start(bf16[8,2,224,128]{3,2,1,0:T(8,128)(2,1)} %copy-done.4), calls=%async_computation.2 | async-start | bytes 1835008 | tf_op jit(solution)/shard_map/all_to_all | solution.py:31
  58.8 2.8 %project.1 = (bf16[2,8,128,512]{3,2,1,0:T(8,128)(2,1)S(1)}, f32[2,232,128]{2,1,0:T(8,128)S(1)}, f32[2,232,128]{2,1,0:T(8,128)S(1)}, f32[2,232,128]{2,1,0:T(8,128)S(1)}, f32[2,232,128]{2,1,0:T(8,128)S(1)}) custom-call(s32[4]{0:T(128)S(1)} %pad_add_fusion.at_ref, bf16[8,2,224,128]{3,2,1,0:T(8,128)(2,1)S(1)} %copy-done.3, ...), custom_call_target="tpu_custom_call" | custom-call | flops 469762048 | bytes 4194304 | tf_op jit(solution)/shard_map/project/pallas_call | solution.py:202
  62.9 2.6 %collective-permute-start.5 = (f32[2,232,128]{2,1,0:T(8,128)S(1)}, f32[2,232,128]{2,1,0:T(8,128)S(1)}, u32[]{:S(2)}, u32[]{:S(2)}) collective-permute-start(f32[2,232,128]{2,1,0:T(8,128)S(1)} %get-tuple-element.37), channel_id=1, source_target_pairs={{0,16},{8,24},{16,0},{24,8},{1,17},{9,25},{17,1},{25,9},{2,18},{10... | collective-permute-start | bytes 712712 | tf_op jit(solution)/shard_map/ppermute | solution.py:27
  67.4 1.5 collective-permute-start.7
  68.9 2.1 %collective-permute-start.8 = (f32[64,224]{1,0:T(8,128)S(1)}, f32[64,224]{1,0:T(8,128)S(1)}, u32[]{:S(2)}, u32[]{:S(2)}) collective-permute-start(f32[64,224]{1,0:T(8,128)S(1)} %get-tuple-element.41), channel_id=1, source_target_pairs={{0,2},{1,3},{2,4},{3,5},{4,6},{5,7},{6,0},{7,1},{8,10},{9,11},{10,... | collective-permute-start | bytes 172040 | tf_op jit(solution)/shard_map/ppermute | solution.py:27
  71.0 5.5 %collective-permute-done.7.refs_1_ = f32[64,224]{1,0:T(8,128)S(1)} collective-permute-done((f32[64,224]{1,0:T(8,128)S(1)}, f32[64,224]{1,0:T(8,128)S(1)}, u32[]{:S(2)}, u32[]{:S(2)}) %collective-permute-start.7) | collective-permute-done | bytes 57376 | tf_op jit(solution)/shard_map/ppermute | solution.py:27
  76.5 3.3 %collective-permute-start.9 = (f32[64,224]{1,0:T(8,128)S(1)}, f32[64,224]{1,0:T(8,128)S(1)}, u32[]{:S(2)}, u32[]{:S(2)}) collective-permute-start(f32[64,224]{1,0:T(8,128)S(1)} %get-tuple-element.42), channel_id=1, source_target_pairs={{0,3},{1,4},{2,5},{3,6},{4,7},{5,0},{6,1},{7,2},{8,11},{9,12},{10,... | collective-permute-start | bytes 172040 | tf_op jit(solution)/shard_map/ppermute | solution.py:27
  79.8 3.0 %collective-permute-done.8.refs_2_ = f32[64,224]{1,0:T(8,128)S(1)} collective-permute-done((f32[64,224]{1,0:T(8,128)S(1)}, f32[64,224]{1,0:T(8,128)S(1)}, u32[]{:S(2)}, u32[]{:S(2)}) %collective-permute-start.8) | collective-permute-done | bytes 57376 | tf_op jit(solution)/shard_map/ppermute | solution.py:27
  82.8 2.6 %collective-permute-start.10 = (f32[64,224]{1,0:T(8,128)S(1)}, f32[64,224]{1,0:T(8,128)S(1)}, u32[]{:S(2)}, u32[]{:S(2)}) collective-permute-start(f32[64,224]{1,0:T(8,128)S(1)} %get-tuple-element.43), channel_id=1, source_target_pairs={{0,4},{1,5},{2,6},{3,7},{4,0},{5,1},{6,2},{7,3},{8,12},{9,13},{10,... | collective-permute-start | bytes 172040 | tf_op jit(solution)/shard_map/ppermute | solution.py:27
  85.4 2.1 %collective-permute-start.11 = (f32[64,224]{1,0:T(8,128)S(1)}, f32[64,224]{1,0:T(8,128)S(1)}, u32[]{:S(2)}, u32[]{:S(2)}) collective-permute-start(f32[64,224]{1,0:T(8,128)S(1)} %get-tuple-element.44), channel_id=1, source_target_pairs={{0,5},{1,6},{2,7},{3,0},{4,1},{5,2},{6,3},{7,4},{8,13},{9,14},{10,... | collective-permute-start | bytes 172040 | tf_op jit(solution)/shard_map/ppermute | solution.py:27
  88.9 4.1 %collective-permute-start.13 = (f32[64,224]{1,0:T(8,128)S(1)}, f32[64,224]{1,0:T(8,128)S(1)}, u32[]{:S(2)}, u32[]{:S(2)}) collective-permute-start(f32[64,224]{1,0:T(8,128)S(1)} %get-tuple-element.46), channel_id=1, source_target_pairs={{0,7},{1,0},{2,1},{3,2},{4,3},{5,4},{6,5},{7,6},{8,15},{9,8},{10,9... | collective-permute-start | bytes 172040 | tf_op jit(solution)/shard_map/ppermute | solution.py:27
  93.1 3.5 %collective-permute-done.12.refs_6_ = f32[64,224]{1,0:T(8,128)S(1)} collective-permute-done((f32[64,224]{1,0:T(8,128)S(1)}, f32[64,224]{1,0:T(8,128)S(1)}, u32[]{:S(2)}, u32[]{:S(2)}) %collective-permute-start.12) | collective-permute-done | bytes 57376 | tf_op jit(solution)/shard_map/ppermute | solution.py:27
  96.5 2.7 %collective-permute-done.13.refs_7_ = f32[64,224]{1,0:T(8,128)S(1)} collective-permute-done((f32[64,224]{1,0:T(8,128)S(1)}, f32[64,224]{1,0:T(8,128)S(1)}, u32[]{:S(2)}, u32[]{:S(2)}) %collective-permute-start.13) | collective-permute-done | bytes 57376 | tf_op jit(solution)/shard_map/ppermute | solution.py:27
  99.2 1.6 moments.1
  100.7 2.7 %collective-permute-start.16 = (bf16[2,224,128]{2,1,0:T(8,128)(2,1)S(1)}, bf16[2,224,128]{2,1,0:T(8,128)(2,1)S(1)}, u32[]{:S(2)}, u32[]{:S(2)}) collective-permute-start(bf16[2,224,128]{2,1,0:T(8,128)(2,1)S(1)} %get-tuple-element.47.u0), channel_id=1, source_target_pairs={{0,24},{8,0},{16,8},{24,16},{1,25},{9,1},{17,9},{25,17},{2,26},{10... | collective-permute-start | bytes 344072 | tf_op jit(solution)/shard_map/ppermute | solution.py:27
  105.5 3.2 %collective-permute-done.15.u2 = bf16[2,224,128]{2,1,0:T(8,128)(2,1)S(1)} collective-permute-done((bf16[2,224,128]{2,1,0:T(8,128)(2,1)S(1)}, bf16[2,224,128]{2,1,0:T(8,128)(2,1)S(1)}, u32[]{:S(2)}, u32[]{:S(2)}) %collective-permute-start.15) | collective-permute-done | bytes 114720 | tf_op jit(solution)/shard_map/ppermute | solution.py:27
  108.7 2.9 %collective-permute-done.14.u1 = bf16[2,224,128]{2,1,0:T(8,128)(2,1)S(1)} collective-permute-done((bf16[2,224,128]{2,1,0:T(8,128)(2,1)S(1)}, bf16[2,224,128]{2,1,0:T(8,128)(2,1)S(1)}, u32[]{:S(2)}, u32[]{:S(2)}) %collective-permute-start.14) | collective-permute-done | bytes 114720 | tf_op jit(solution)/shard_map/ppermute | solution.py:27
  111.6 3.2 %back.2 = bf16[8,224,128]{2,1,0:T(8,128)(2,1)} custom-call(s32[4]{0:T(128)S(1)} %pad_add_fusion.at_ref, bf16[2,8,128,512]{3,2,1,0:T(8,128)(2,1)S(1)} %get-tuple-element.33.basis_ref, bf16[8,2,224,128]{3,2,1,0:T(8,128)(2,1)S(1)} %all-to-all-done.2.w_ref, bf16[2,224,128]{2,1,0:T(8,128)(2,1)S(1)} %get-tuple-element.47.u0, ...), custom_call_target="tpu_custom_call" | custom-call | flops 234881024 | bytes 3145728 | tf_op jit(solution)/shard_map/back/pallas_call | solution.py:293
  114.8 5.9 %all-to-all-start.3 = ((bf16[8,224,128]{2,1,0:T(8,128)(2,1)}), bf16[8,224,128]{2,1,0:T(8,128)(2,1)}, u32[]{:S(2)}, u32[]{:S(2)}) async-start(bf16[8,224,128]{2,1,0:T(8,128)(2,1)} %back.2), calls=%async_computation.3 | async-start | bytes 917504 | tf_op jit(solution)/shard_map/all_to_all | solution.py:31
  121.8 1.5 collective-permute-start.23
  123.4 2.1 %collective-permute-start.24 = (bf16[224,128]{1,0:T(8,128)(2,1)S(1)}, bf16[224,128]{1,0:T(8,128)(2,1)S(1)}, u32[]{:S(2)}, u32[]{:S(2)}) collective-permute-start(bf16[224,128]{1,0:T(8,128)(2,1)S(1)} %get-tuple-element.50), channel_id=1, source_target_pairs={{0,2},{1,3},{2,4},{3,5},{4,6},{5,7},{6,0},{7,1},{8,10},{9,11},{10,... | collective-permute-start | bytes 172040 | tf_op jit(solution)/shard_map/ppermute | solution.py:27
  125.5 2.4 %collective-permute-start.25 = (bf16[224,128]{1,0:T(8,128)(2,1)S(1)}, bf16[224,128]{1,0:T(8,128)(2,1)S(1)}, u32[]{:S(2)}, u32[]{:S(2)}) collective-permute-start(bf16[224,128]{1,0:T(8,128)(2,1)S(1)} %get-tuple-element.51), channel_id=1, source_target_pairs={{0,3},{1,4},{2,5},{3,6},{4,7},{5,0},{6,1},{7,2},{8,11},{9,12},{10,... | collective-permute-start | bytes 172040 | tf_op jit(solution)/shard_map/ppermute | solution.py:27
  127.9 2.1 %collective-permute-start.26 = (bf16[224,128]{1,0:T(8,128)(2,1)S(1)}, bf16[224,128]{1,0:T(8,128)(2,1)S(1)}, u32[]{:S(2)}, u32[]{:S(2)}) collective-permute-start(bf16[224,128]{1,0:T(8,128)(2,1)S(1)} %get-tuple-element.52), channel_id=1, source_target_pairs={{0,4},{1,5},{2,6},{3,7},{4,0},{5,1},{6,2},{7,3},{8,12},{9,13},{10,... | collective-permute-start | bytes 172040 | tf_op jit(solution)/shard_map/ppermute | solution.py:27
  129.9 2.4 %collective-permute-start.27 = (bf16[224,128]{1,0:T(8,128)(2,1)S(1)}, bf16[224,128]{1,0:T(8,128)(2,1)S(1)}, u32[]{:S(2)}, u32[]{:S(2)}) collective-permute-start(bf16[224,128]{1,0:T(8,128)(2,1)S(1)} %get-tuple-element.53), channel_id=1, source_target_pairs={{0,5},{1,6},{2,7},{3,0},{4,1},{5,2},{6,3},{7,4},{8,13},{9,14},{10,... | collective-permute-start | bytes 172040 | tf_op jit(solution)/shard_map/ppermute | solution.py:27
  133.1 2.5 %collective-permute-start.28 = (bf16[224,128]{1,0:T(8,128)(2,1)S(1)}, bf16[224,128]{1,0:T(8,128)(2,1)S(1)}, u32[]{:S(2)}, u32[]{:S(2)}) collective-permute-start(bf16[224,128]{1,0:T(8,128)(2,1)S(1)} %get-tuple-element.54), channel_id=1, source_target_pairs={{0,6},{1,7},{2,0},{3,1},{4,2},{5,3},{6,4},{7,5},{8,14},{9,15},{10,... | collective-permute-start | bytes 172040 | tf_op jit(solution)/shard_map/ppermute | solution.py:27
  135.6 2.0 collective-permute-done.24.refs_2_
  138.9 6.2 %collective-permute-done.26.refs_4_ = bf16[224,128]{1,0:T(8,128)(2,1)S(1)} collective-permute-done((bf16[224,128]{1,0:T(8,128)(2,1)S(1)}, bf16[224,128]{1,0:T(8,128)(2,1)S(1)}, u32[]{:S(2)}, u32[]{:S(2)}) %collective-permute-start.26) | collective-permute-done | bytes 57376 | tf_op jit(solution)/shard_map/ppermute | solution.py:27
  145.9 2.3 %collective-permute-start.31 = (bf16[128,1792]{1,0:T(8,128)(2,1)S(1)}, bf16[128,1792]{1,0:T(8,128)(2,1)S(1)}, u32[]{:S(2)}, u32[]{:S(2)}) collective-permute-start(bf16[128,1792]{1,0:T(8,128)(2,1)S(1)} %turn.1.refs_4_), channel_id=1, source_target_pairs={{0,192},{64,0},{128,64},{192,128},{1,193},{65,1},{129,65},{193,129... | collective-permute-start | bytes 1376264 | tf_op jit(solution)/shard_map/ppermute | solution.py:27
  148.2 1.6 collective-permute-start.32
  152.7 4.2 %collective-permute-done.31.refs_6_ = bf16[128,1792]{1,0:T(8,128)(2,1)S(1)} collective-permute-done((bf16[128,1792]{1,0:T(8,128)(2,1)S(1)}, bf16[128,1792]{1,0:T(8,128)(2,1)S(1)}, u32[]{:S(2)}, u32[]{:S(2)}) %collective-permute-start.31) | collective-permute-done | bytes 458784 | tf_op jit(solution)/shard_map/ppermute | solution.py:27
  156.9 3.9 %collective-permute-start.34 = (bf16[128,1792]{1,0:T(8,128)(2,1)S(1)}, bf16[128,1792]{1,0:T(8,128)(2,1)}, u32[]{:S(2)}, u32[]{:S(2)}) collective-permute-start(bf16[128,1792]{1,0:T(8,128)(2,1)S(1)} %collective-permute-done.31.refs_6_), channel_id=1, source_target_pairs={{0,32},{32,0},{1,33},{33,1},{2,34},{34,2},{3,35},{35,3},{4,36},{36... | collective-permute-start | bytes 1376264 | tf_op jit(solution)/shard_map/ppermute | solution.py:27
  161.5 5.1 %collective-permute-done.19.refs_2_ = bf16[128,1792]{1,0:T(8,128)(2,1)S(1)} collective-permute-done((bf16[128,1792]{1,0:T(8,128)(2,1)S(1)}, bf16[128,1792]{1,0:T(8,128)(2,1)S(1)}, u32[]{:S(2)}, u32[]{:S(2)}) %collective-permute-start.19) | collective-permute-done | bytes 458784 | tf_op jit(solution)/shard_map/ppermute | solution.py:27
  166.7 2.1 %collective-permute-start.37 = (bf16[128,1792]{1,0:T(8,128)(2,1)S(1)}, bf16[128,1792]{1,0:T(8,128)(2,1)}, u32[]{:S(2)}, u32[]{:S(2)}) collective-permute-start(bf16[128,1792]{1,0:T(8,128)(2,1)S(1)} %collective-permute-done.19.refs_2_), channel_id=1, source_target_pairs={{0,32},{32,0},{1,33},{33,1},{2,34},{34,2},{3,35},{35,3},{4,36},{36... | collective-permute-start | bytes 1376264 | tf_op jit(solution)/shard_map/ppermute | solution.py:27
  168.8 3.5 %all-to-all-start.4 = ((f32[8,64,224]{2,1,0:T(8,128)}), f32[8,64,224]{2,1,0:T(8,128)S(1)}, u32[]{:S(2)}, u32[]{:S(2)}) async-start(f32[8,64,224]{2,1,0:T(8,128)} %get-tuple-element.60), calls=%async_computation.4 | async-start | bytes 1048576 | tf_op jit(solution)/shard_map/all_to_all | solution.py:31
  172.3 2.2 %collective-permute-done.30.refs_5_ = bf16[128,1792]{1,0:T(8,128)(2,1)S(1)} collective-permute-done((bf16[128,1792]{1,0:T(8,128)(2,1)S(1)}, bf16[128,1792]{1,0:T(8,128)(2,1)S(1)}, u32[]{:S(2)}, u32[]{:S(2)}) %collective-permute-start.30) | collective-permute-done | bytes 458784 | tf_op jit(solution)/shard_map/ppermute | solution.py:27
  177.2 5.7 %collective-permute-done.20.refs_1_ = bf16[64,1792]{1,0:T(8,128)(2,1)S(1)} collective-permute-done((bf16[64,1792]{1,0:T(8,128)(2,1)S(1)}, bf16[64,1792]{1,0:T(8,128)(2,1)S(1)}, u32[]{:S(2)}, u32[]{:S(2)}) %collective-permute-start.20) | collective-permute-done | bytes 229408 | tf_op jit(solution)/shard_map/ppermute | solution.py:27
  187.2 2.9 %place.3.refs_10_ = bf16[2,128,14336]{2,1,0:T(8,128)(2,1)} custom-call(s32[4]{0:T(128)S(1)} %pad_add_fusion.at_ref, bf16[128,1792]{1,0:T(8,128)(2,1)S(1)} %bitcast.13, bf16[128,1792]{1,0:T(8,128)(2,1)S(1)} %collective-permute-done.17.refs_1_, bf16[128,1792]{1,0:T(8,128)(2,1)S(1)} %collective-permute-done.19.refs_2_, ...), custom_call_target="tpu_custom_call" | custom-call | flops 2000000000 | bytes 5505024 | tf_op jit(solution)/shard_map/place/pallas_call | solution.py:354
  190.1 3.0 %place.4.refs_4_ = bf16[2,128,14336]{2,1,0:T(8,128)(2,1)} custom-call(s32[4]{0:T(128)S(1)} %pad_add_fusion.at_ref, bf16[64,1792]{1,0:T(8,128)(2,1)S(1)} %collective-permute-done.18.refs_0_, bf16[64,1792]{1,0:T(8,128)(2,1)S(1)} %collective-permute-done.20.refs_1_, ...), custom_call_target="tpu_custom_call", output_to_operand_aliasing={{}: (11, {})} | custom-call | flops 2000000000 | bytes 7340032 | tf_op jit(solution)/shard_map/place/pallas_call | solution.py:354
  193.6 1.6 collective-permute-start.40
  196.8 1.9 place.5
  (93 shorter events, 34.6 us)
Async XLA Ops:
  2.8 10.4 %copy-start.8 = (bf16[2,128,1792]{2,1,0:T(8,128)(2,1)S(1)}, bf16[2,128,1792]{2,1,0:T(8,128)(2,1)}, u32[]{:S(2)}) copy-start(bf16[2,128,1792]{2,1,0:T(8,128)(2,1)} %v_ref.4) | copy-start | bytes 2752516
  4.3 20.3 %all-to-all-start.1 = ((bf16[8,144,128]{2,1,0:T(8,128)(2,1)}), bf16[8,144,128]{2,1,0:T(8,128)(2,1)S(1)}, u32[]{:S(2)}, u32[]{:S(2)}) async-start(bf16[8,144,128]{2,1,0:T(8,128)(2,1)} %pieces.1), calls=%async_computation.1 | async-start | bytes 589824 | tf_op jit(solution)/shard_map/all_to_all | solution.py:31
  24.5 28.2 %all-to-all-start = ((bf16[8,2,224,128]{3,2,1,0:T(8,128)(2,1)}), bf16[8,2,224,128]{3,2,1,0:T(8,128)(2,1)S(1)}, u32[]{:S(2)}, u32[]{:S(2)}) async-start(bf16[8,2,224,128]{3,2,1,0:T(8,128)(2,1)} %pack.2), calls=%async_computation | async-start | bytes 1835008 | tf_op jit(solution)/shard_map/all_to_all | solution.py:31
  28.1 7.9 %collective-permute-start.2 = (bf16[8,144,128]{2,1,0:T(8,128)(2,1)S(1)}, bf16[8,144,128]{2,1,0:T(8,128)(2,1)S(1)}, u32[]{:S(2)}, u32[]{:S(2)}) collective-permute-start(bf16[8,144,128]{2,1,0:T(8,128)(2,1)S(1)} %all-to-all-done.1), channel_id=1, source_target_pairs={{0,192},{64,0},{128,64},{192,128},{1,193},{65,1},{129,65},{193,129... | collective-permute-start | bytes 884744 | tf_op jit(solution)/shard_map/ppermute | solution.py:27
  30.6 7.6 %collective-permute-start.1 = (bf16[8,144,128]{2,1,0:T(8,128)(2,1)S(1)}, bf16[8,144,128]{2,1,0:T(8,128)(2,1)S(1)}, u32[]{:S(2)}, u32[]{:S(2)}) collective-permute-start(bf16[8,144,128]{2,1,0:T(8,128)(2,1)S(1)} %all-to-all-done.1), channel_id=1, source_target_pairs={{0,128},{64,192},{128,0},{192,64},{1,129},{65,193},{129,1},{193,65... | collective-permute-start | bytes 884744 | tf_op jit(solution)/shard_map/ppermute | solution.py:27
  31.2 16.2 %collective-permute-start = (bf16[8,144,128]{2,1,0:T(8,128)(2,1)S(1)}, bf16[8,144,128]{2,1,0:T(8,128)(2,1)S(1)}, u32[]{:S(2)}, u32[]{:S(2)}) collective-permute-start(bf16[8,144,128]{2,1,0:T(8,128)(2,1)S(1)} %all-to-all-done.1), channel_id=1, source_target_pairs={{0,64},{64,128},{128,192},{192,0},{1,65},{65,129},{129,193},{193,1... | collective-permute-start | bytes 884744 | tf_op jit(solution)/shard_map/ppermute | solution.py:27
  47.6 8.8 %collective-permute-start.3 = (bf16[4,8,144,128]{3,2,1,0:T(8,128)(2,1)S(1)}, bf16[4,8,144,128]{3,2,1,0:T(8,128)(2,1)}, u32[]{:S(2)}, u32[]{:S(2)}) collective-permute-start(bf16[4,8,144,128]{3,2,1,0:T(8,128)(2,1)S(1)} %pad_maximum_fusion.own_ref), channel_id=1, source_target_pairs={{0,32},{32,0},{1,33},{33,1},{2,34},{34,2},{3,35},{35,3},{4,36},{36... | collective-permute-start | bytes 3538952 | tf_op jit(solution)/shard_map/ppermute | solution.py:27
  52.8 58.9 %all-to-all-start.2 = ((bf16[8,2,224,128]{3,2,1,0:T(8,128)(2,1)}), bf16[8,2,224,128]{3,2,1,0:T(8,128)(2,1)S(1)}, u32[]{:S(2)}, u32[]{:S(2)}) async-start(bf16[8,2,224,128]{3,2,1,0:T(8,128)(2,1)} %copy-done.4), calls=%async_computation.2 | async-start | bytes 1835008 | tf_op jit(solution)/shard_map/all_to_all | solution.py:31
  61.6 23.8 %collective-permute-start.4 = (f32[2,232,128]{2,1,0:T(8,128)S(1)}, f32[2,232,128]{2,1,0:T(8,128)S(1)}, u32[]{:S(2)}, u32[]{:S(2)}) collective-permute-start(f32[2,232,128]{2,1,0:T(8,128)S(1)} %get-tuple-element.36), channel_id=1, source_target_pairs={{0,8},{8,16},{16,24},{24,0},{1,9},{9,17},{17,25},{25,1},{2,10},{10... | collective-permute-start | bytes 712712 | tf_op jit(solution)/shard_map/ppermute | solution.py:27
  62.9 24.5 %collective-permute-start.5 = (f32[2,232,128]{2,1,0:T(8,128)S(1)}, f32[2,232,128]{2,1,0:T(8,128)S(1)}, u32[]{:S(2)}, u32[]{:S(2)}) collective-permute-start(f32[2,232,128]{2,1,0:T(8,128)S(1)} %get-tuple-element.37), channel_id=1, source_target_pairs={{0,16},{8,24},{16,0},{24,8},{1,17},{9,25},{17,1},{25,9},{2,18},{10... | collective-permute-start | bytes 712712 | tf_op jit(solution)/shard_map/ppermute | solution.py:27
  65.5 23.3 %collective-permute-start.6 = (f32[2,232,128]{2,1,0:T(8,128)S(1)}, f32[2,232,128]{2,1,0:T(8,128)S(1)}, u32[]{:S(2)}, u32[]{:S(2)}) collective-permute-start(f32[2,232,128]{2,1,0:T(8,128)S(1)} %get-tuple-element.38), channel_id=1, source_target_pairs={{0,24},{8,0},{16,8},{24,16},{1,25},{9,1},{17,9},{25,17},{2,26},{10... | collective-permute-start | bytes 712712 | tf_op jit(solution)/shard_map/ppermute | solution.py:27
  67.4 9.1 %collective-permute-start.7 = (f32[64,224]{1,0:T(8,128)S(1)}, f32[64,224]{1,0:T(8,128)S(1)}, u32[]{:S(2)}, u32[]{:S(2)}) collective-permute-start(f32[64,224]{1,0:T(8,128)S(1)} %get-tuple-element.40), channel_id=1, source_target_pairs={{0,1},{1,2},{2,3},{3,4},{4,5},{5,6},{6,7},{7,0},{8,9},{9,10},{10,1... | collective-permute-start | bytes 172040 | tf_op jit(solution)/shard_map/ppermute | solution.py:27
  68.9 13.9 %collective-permute-start.8 = (f32[64,224]{1,0:T(8,128)S(1)}, f32[64,224]{1,0:T(8,128)S(1)}, u32[]{:S(2)}, u32[]{:S(2)}) collective-permute-start(f32[64,224]{1,0:T(8,128)S(1)} %get-tuple-element.41), channel_id=1, source_target_pairs={{0,2},{1,3},{2,4},{3,5},{4,6},{5,7},{6,0},{7,1},{8,10},{9,11},{10,... | collective-permute-start | bytes 172040 | tf_op jit(solution)/shard_map/ppermute | solution.py:27
  76.5 16.6 %collective-permute-start.9 = (f32[64,224]{1,0:T(8,128)S(1)}, f32[64,224]{1,0:T(8,128)S(1)}, u32[]{:S(2)}, u32[]{:S(2)}) collective-permute-start(f32[64,224]{1,0:T(8,128)S(1)} %get-tuple-element.42), channel_id=1, source_target_pairs={{0,3},{1,4},{2,5},{3,6},{4,7},{5,0},{6,1},{7,2},{8,11},{9,12},{10,... | collective-permute-start | bytes 172040 | tf_op jit(solution)/shard_map/ppermute | solution.py:27
  82.8 10.2 %collective-permute-start.10 = (f32[64,224]{1,0:T(8,128)S(1)}, f32[64,224]{1,0:T(8,128)S(1)}, u32[]{:S(2)}, u32[]{:S(2)}) collective-permute-start(f32[64,224]{1,0:T(8,128)S(1)} %get-tuple-element.43), channel_id=1, source_target_pairs={{0,4},{1,5},{2,6},{3,7},{4,0},{5,1},{6,2},{7,3},{8,12},{9,13},{10,... | collective-permute-start | bytes 172040 | tf_op jit(solution)/shard_map/ppermute | solution.py:27
  85.4 7.7 %collective-permute-start.11 = (f32[64,224]{1,0:T(8,128)S(1)}, f32[64,224]{1,0:T(8,128)S(1)}, u32[]{:S(2)}, u32[]{:S(2)}) collective-permute-start(f32[64,224]{1,0:T(8,128)S(1)} %get-tuple-element.44), channel_id=1, source_target_pairs={{0,5},{1,6},{2,7},{3,0},{4,1},{5,2},{6,3},{7,4},{8,13},{9,14},{10,... | collective-permute-start | bytes 172040 | tf_op jit(solution)/shard_map/ppermute | solution.py:27
  87.4 9.1 %collective-permute-start.12 = (f32[64,224]{1,0:T(8,128)S(1)}, f32[64,224]{1,0:T(8,128)S(1)}, u32[]{:S(2)}, u32[]{:S(2)}) collective-permute-start(f32[64,224]{1,0:T(8,128)S(1)} %get-tuple-element.45), channel_id=1, source_target_pairs={{0,6},{1,7},{2,0},{3,1},{4,2},{5,3},{6,4},{7,5},{8,14},{9,15},{10,... | collective-permute-start | bytes 172040 | tf_op jit(solution)/shard_map/ppermute | solution.py:27
  88.9 10.3 %collective-permute-start.13 = (f32[64,224]{1,0:T(8,128)S(1)}, f32[64,224]{1,0:T(8,128)S(1)}, u32[]{:S(2)}, u32[]{:S(2)}) collective-permute-start(f32[64,224]{1,0:T(8,128)S(1)} %get-tuple-element.46), channel_id=1, source_target_pairs={{0,7},{1,0},{2,1},{3,2},{4,3},{5,4},{6,5},{7,6},{8,15},{9,8},{10,9... | collective-permute-start | bytes 172040 | tf_op jit(solution)/shard_map/ppermute | solution.py:27
  100.7 4.8 %collective-permute-start.16 = (bf16[2,224,128]{2,1,0:T(8,128)(2,1)S(1)}, bf16[2,224,128]{2,1,0:T(8,128)(2,1)S(1)}, u32[]{:S(2)}, u32[]{:S(2)}) collective-permute-start(bf16[2,224,128]{2,1,0:T(8,128)(2,1)S(1)} %get-tuple-element.47.u0), channel_id=1, source_target_pairs={{0,24},{8,0},{16,8},{24,16},{1,25},{9,1},{17,9},{25,17},{2,26},{10... | collective-permute-start | bytes 344072 | tf_op jit(solution)/shard_map/ppermute | solution.py:27
  103.5 5.2 %collective-permute-start.15 = (bf16[2,224,128]{2,1,0:T(8,128)(2,1)S(1)}, bf16[2,224,128]{2,1,0:T(8,128)(2,1)S(1)}, u32[]{:S(2)}, u32[]{:S(2)}) collective-permute-start(bf16[2,224,128]{2,1,0:T(8,128)(2,1)S(1)} %get-tuple-element.47.u0), channel_id=1, source_target_pairs={{0,16},{8,24},{16,0},{24,8},{1,17},{9,25},{17,1},{25,9},{2,18},{10... | collective-permute-start | bytes 344072 | tf_op jit(solution)/shard_map/ppermute | solution.py:27
  103.8 7.8 %collective-permute-start.14 = (bf16[2,224,128]{2,1,0:T(8,128)(2,1)S(1)}, bf16[2,224,128]{2,1,0:T(8,128)(2,1)S(1)}, u32[]{:S(2)}, u32[]{:S(2)}) collective-permute-start(bf16[2,224,128]{2,1,0:T(8,128)(2,1)S(1)} %get-tuple-element.47.u0), channel_id=1, source_target_pairs={{0,8},{8,16},{16,24},{24,0},{1,9},{9,17},{17,25},{25,1},{2,10},{10... | collective-permute-start | bytes 344072 | tf_op jit(solution)/shard_map/ppermute | solution.py:27
  114.8 35.1 %all-to-all-start.3 = ((bf16[8,224,128]{2,1,0:T(8,128)(2,1)}), bf16[8,224,128]{2,1,0:T(8,128)(2,1)}, u32[]{:S(2)}, u32[]{:S(2)}) async-start(bf16[8,224,128]{2,1,0:T(8,128)(2,1)} %back.2), calls=%async_computation.3 | async-start | bytes 917504 | tf_op jit(solution)/shard_map/all_to_all | solution.py:31
  121.8 11.2 %collective-permute-start.23 = (bf16[224,128]{1,0:T(8,128)(2,1)S(1)}, bf16[224,128]{1,0:T(8,128)(2,1)S(1)}, u32[]{:S(2)}, u32[]{:S(2)}) collective-permute-start(bf16[224,128]{1,0:T(8,128)(2,1)S(1)} %get-tuple-element.49), channel_id=1, source_target_pairs={{0,1},{1,2},{2,3},{3,4},{4,5},{5,6},{6,7},{7,0},{8,9},{9,10},{10,1... | collective-permute-start | bytes 172040 | tf_op jit(solution)/shard_map/ppermute | solution.py:27
  123.4 14.2 %collective-permute-start.24 = (bf16[224,128]{1,0:T(8,128)(2,1)S(1)}, bf16[224,128]{1,0:T(8,128)(2,1)S(1)}, u32[]{:S(2)}, u32[]{:S(2)}) collective-permute-start(bf16[224,128]{1,0:T(8,128)(2,1)S(1)} %get-tuple-element.50), channel_id=1, source_target_pairs={{0,2},{1,3},{2,4},{3,5},{4,6},{5,7},{6,0},{7,1},{8,10},{9,11},{10,... | collective-permute-start | bytes 172040 | tf_op jit(solution)/shard_map/ppermute | solution.py:27
  125.5 13.4 %collective-permute-start.25 = (bf16[224,128]{1,0:T(8,128)(2,1)S(1)}, bf16[224,128]{1,0:T(8,128)(2,1)S(1)}, u32[]{:S(2)}, u32[]{:S(2)}) collective-permute-start(bf16[224,128]{1,0:T(8,128)(2,1)S(1)} %get-tuple-element.51), channel_id=1, source_target_pairs={{0,3},{1,4},{2,5},{3,6},{4,7},{5,0},{6,1},{7,2},{8,11},{9,12},{10,... | collective-permute-start | bytes 172040 | tf_op jit(solution)/shard_map/ppermute | solution.py:27
  127.9 17.3 %collective-permute-start.26 = (bf16[224,128]{1,0:T(8,128)(2,1)S(1)}, bf16[224,128]{1,0:T(8,128)(2,1)S(1)}, u32[]{:S(2)}, u32[]{:S(2)}) collective-permute-start(bf16[224,128]{1,0:T(8,128)(2,1)S(1)} %get-tuple-element.52), channel_id=1, source_target_pairs={{0,4},{1,5},{2,6},{3,7},{4,0},{5,1},{6,2},{7,3},{8,12},{9,13},{10,... | collective-permute-start | bytes 172040 | tf_op jit(solution)/shard_map/ppermute | solution.py:27
  129.9 15.2 %collective-permute-start.27 = (bf16[224,128]{1,0:T(8,128)(2,1)S(1)}, bf16[224,128]{1,0:T(8,128)(2,1)S(1)}, u32[]{:S(2)}, u32[]{:S(2)}) collective-permute-start(bf16[224,128]{1,0:T(8,128)(2,1)S(1)} %get-tuple-element.53), channel_id=1, source_target_pairs={{0,5},{1,6},{2,7},{3,0},{4,1},{5,2},{6,3},{7,4},{8,13},{9,14},{10,... | collective-permute-start | bytes 172040 | tf_op jit(solution)/shard_map/ppermute | solution.py:27
  133.1 12.0 %collective-permute-start.28 = (bf16[224,128]{1,0:T(8,128)(2,1)S(1)}, bf16[224,128]{1,0:T(8,128)(2,1)S(1)}, u32[]{:S(2)}, u32[]{:S(2)}) collective-permute-start(bf16[224,128]{1,0:T(8,128)(2,1)S(1)} %get-tuple-element.54), channel_id=1, source_target_pairs={{0,6},{1,7},{2,0},{3,1},{4,2},{5,3},{6,4},{7,5},{8,14},{9,15},{10,... | collective-permute-start | bytes 172040 | tf_op jit(solution)/shard_map/ppermute | solution.py:27
  137.6 7.5 %collective-permute-start.29 = (bf16[224,128]{1,0:T(8,128)(2,1)S(1)}, bf16[224,128]{1,0:T(8,128)(2,1)S(1)}, u32[]{:S(2)}, u32[]{:S(2)}) collective-permute-start(bf16[224,128]{1,0:T(8,128)(2,1)S(1)} %get-tuple-element.55), channel_id=1, source_target_pairs={{0,7},{1,0},{2,1},{3,2},{4,3},{5,4},{6,5},{7,6},{8,15},{9,8},{10,9... | collective-permute-start | bytes 172040 | tf_op jit(solution)/shard_map/ppermute | solution.py:27
  145.9 11.0 %collective-permute-start.31 = (bf16[128,1792]{1,0:T(8,128)(2,1)S(1)}, bf16[128,1792]{1,0:T(8,128)(2,1)S(1)}, u32[]{:S(2)}, u32[]{:S(2)}) collective-permute-start(bf16[128,1792]{1,0:T(8,128)(2,1)S(1)} %turn.1.refs_4_), channel_id=1, source_target_pairs={{0,192},{64,0},{128,64},{192,128},{1,193},{65,1},{129,65},{193,129... | collective-permute-start | bytes 1376264 | tf_op jit(solution)/shard_map/ppermute | solution.py:27
  148.2 12.6 %collective-permute-start.32 = (bf16[128,1792]{1,0:T(8,128)(2,1)S(1)}, bf16[128,1792]{1,0:T(8,128)(2,1)S(1)}, u32[]{:S(2)}, u32[]{:S(2)}) collective-permute-start(bf16[128,1792]{1,0:T(8,128)(2,1)S(1)} %turn.1.refs_4_), channel_id=1, source_target_pairs={{0,32},{32,0},{1,33},{33,1},{2,34},{34,2},{3,35},{35,3},{4,36},{36... | collective-permute-start | bytes 1376264 | tf_op jit(solution)/shard_map/ppermute | solution.py:27
  151.1 15.6 %collective-permute-start.19 = (bf16[128,1792]{1,0:T(8,128)(2,1)S(1)}, bf16[128,1792]{1,0:T(8,128)(2,1)S(1)}, u32[]{:S(2)}, u32[]{:S(2)}) collective-permute-start(bf16[128,1792]{1,0:T(8,128)(2,1)S(1)} %bitcast.10), channel_id=1, source_target_pairs={{0,192},{64,0},{128,64},{192,128},{1,193},{65,1},{129,65},{193,129... | collective-permute-start | bytes 1376264 | tf_op jit(solution)/shard_map/ppermute | solution.py:27
  151.7 17.1 %collective-permute-start.17 = (bf16[128,1792]{1,0:T(8,128)(2,1)S(1)}, bf16[128,1792]{1,0:T(8,128)(2,1)S(1)}, u32[]{:S(2)}, u32[]{:S(2)}) collective-permute-start(bf16[128,1792]{1,0:T(8,128)(2,1)S(1)} %bitcast.11), channel_id=1, source_target_pairs={{0,64},{64,128},{128,192},{192,0},{1,65},{65,129},{129,193},{193,1... | collective-permute-start | bytes 1376264 | tf_op jit(solution)/shard_map/ppermute | solution.py:27
  152.6 21.9 %collective-permute-start.30 = (bf16[128,1792]{1,0:T(8,128)(2,1)S(1)}, bf16[128,1792]{1,0:T(8,128)(2,1)S(1)}, u32[]{:S(2)}, u32[]{:S(2)}) collective-permute-start(bf16[128,1792]{1,0:T(8,128)(2,1)S(1)} %turn.1.refs_4_), channel_id=1, source_target_pairs={{0,64},{64,128},{128,192},{192,0},{1,65},{65,129},{129,193},{193,1... | collective-permute-start | bytes 1376264 | tf_op jit(solution)/shard_map/ppermute | solution.py:27
  156.9 18.8 %collective-permute-start.34 = (bf16[128,1792]{1,0:T(8,128)(2,1)S(1)}, bf16[128,1792]{1,0:T(8,128)(2,1)}, u32[]{:S(2)}, u32[]{:S(2)}) collective-permute-start(bf16[128,1792]{1,0:T(8,128)(2,1)S(1)} %collective-permute-done.31.refs_6_), channel_id=1, source_target_pairs={{0,32},{32,0},{1,33},{33,1},{2,34},{34,2},{3,35},{35,3},{4,36},{36... | collective-permute-start | bytes 1376264 | tf_op jit(solution)/shard_map/ppermute | solution.py:27
  161.5 14.8 %collective-permute-start.35 = (bf16[128,1792]{1,0:T(8,128)(2,1)S(1)}, bf16[128,1792]{1,0:T(8,128)(2,1)}, u32[]{:S(2)}, u32[]{:S(2)}) collective-permute-start(bf16[128,1792]{1,0:T(8,128)(2,1)S(1)} %bitcast.12), channel_id=1, source_target_pairs={{0,32},{32,0},{1,33},{33,1},{2,34},{34,2},{3,35},{35,3},{4,36},{36... | collective-permute-start | bytes 1376264 | tf_op jit(solution)/shard_map/ppermute | solution.py:27
  166.7 19.0 %collective-permute-start.37 = (bf16[128,1792]{1,0:T(8,128)(2,1)S(1)}, bf16[128,1792]{1,0:T(8,128)(2,1)}, u32[]{:S(2)}, u32[]{:S(2)}) collective-permute-start(bf16[128,1792]{1,0:T(8,128)(2,1)S(1)} %collective-permute-done.19.refs_2_), channel_id=1, source_target_pairs={{0,32},{32,0},{1,33},{33,1},{2,34},{34,2},{3,35},{35,3},{4,36},{36... | collective-permute-start | bytes 1376264 | tf_op jit(solution)/shard_map/ppermute | solution.py:27
  168.8 17.0 %collective-permute-start.36 = (bf16[128,1792]{1,0:T(8,128)(2,1)S(1)}, bf16[128,1792]{1,0:T(8,128)(2,1)}, u32[]{:S(2)}, u32[]{:S(2)}) collective-permute-start(bf16[128,1792]{1,0:T(8,128)(2,1)S(1)} %collective-permute-done.17.refs_1_), channel_id=1, source_target_pairs={{0,32},{32,0},{1,33},{33,1},{2,34},{34,2},{3,35},{35,3},{4,36},{36... | collective-permute-start | bytes 1376264 | tf_op jit(solution)/shard_map/ppermute | solution.py:27
  168.8 26.4 %all-to-all-start.4 = ((f32[8,64,224]{2,1,0:T(8,128)}), f32[8,64,224]{2,1,0:T(8,128)S(1)}, u32[]{:S(2)}, u32[]{:S(2)}) async-start(f32[8,64,224]{2,1,0:T(8,128)} %get-tuple-element.60), calls=%async_computation.4 | async-start | bytes 1048576 | tf_op jit(solution)/shard_map/all_to_all | solution.py:31
  174.6 15.5 %collective-permute-start.33 = (bf16[128,1792]{1,0:T(8,128)(2,1)S(1)}, bf16[128,1792]{1,0:T(8,128)(2,1)S(1)}, u32[]{:S(2)}, u32[]{:S(2)}) collective-permute-start(bf16[128,1792]{1,0:T(8,128)(2,1)S(1)} %collective-permute-done.30.refs_5_), channel_id=1, source_target_pairs={{0,32},{32,0},{1,33},{33,1},{2,34},{34,2},{3,35},{35,3},{4,36},{36... | collective-permute-start | bytes 1376264 | tf_op jit(solution)/shard_map/ppermute | solution.py:27
  175.7 7.2 %collective-permute-start.20 = (bf16[64,1792]{1,0:T(8,128)(2,1)S(1)}, bf16[64,1792]{1,0:T(8,128)(2,1)S(1)}, u32[]{:S(2)}, u32[]{:S(2)}) collective-permute-start(bf16[64,1792]{1,0:T(8,128)(2,1)S(1)} %slice.17), channel_id=1, source_target_pairs={{0,192},{64,0},{128,64},{192,128},{1,193},{65,1},{129,65},{193,129... | collective-permute-start | bytes 688136 | tf_op jit(solution)/shard_map/ppermute | solution.py:27
  176.4 8.0 %collective-permute-start.18 = (bf16[64,1792]{1,0:T(8,128)(2,1)S(1)}, bf16[64,1792]{1,0:T(8,128)(2,1)S(1)}, u32[]{:S(2)}, u32[]{:S(2)}) collective-permute-start(bf16[64,1792]{1,0:T(8,128)(2,1)S(1)} %slice.16), channel_id=1, source_target_pairs={{0,64},{64,128},{128,192},{192,0},{1,65},{65,129},{129,193},{193,1... | collective-permute-start | bytes 688136 | tf_op jit(solution)/shard_map/ppermute | solution.py:27
  182.9 7.2 %collective-permute-start.22 = (bf16[64,1792]{1,0:T(8,128)(2,1)S(1)}, bf16[64,1792]{1,0:T(8,128)(2,1)S(1)}, u32[]{:S(2)}, u32[]{:S(2)}) collective-permute-start(bf16[64,1792]{1,0:T(8,128)(2,1)S(1)} %collective-permute-done.20.refs_1_), channel_id=1, source_target_pairs={{0,32},{32,0},{1,33},{33,1},{2,34},{34,2},{3,35},{35,3},{4,36},{36... | collective-permute-start | bytes 688136 | tf_op jit(solution)/shard_map/ppermute | solution.py:27
  184.4 5.8 %collective-permute-start.21 = (bf16[64,1792]{1,0:T(8,128)(2,1)S(1)}, bf16[64,1792]{1,0:T(8,128)(2,1)S(1)}, u32[]{:S(2)}, u32[]{:S(2)}) collective-permute-start(bf16[64,1792]{1,0:T(8,128)(2,1)S(1)} %collective-permute-done.18.refs_0_), channel_id=1, source_target_pairs={{0,32},{32,0},{1,33},{33,1},{2,34},{34,2},{3,35},{35,3},{4,36},{36... | collective-permute-start | bytes 688136 | tf_op jit(solution)/shard_map/ppermute | solution.py:27
  185.7 7.4 %collective-permute-start.39 = (bf16[64,1792]{1,0:T(8,128)(2,1)S(1)}, bf16[64,1792]{1,0:T(8,128)(2,1)S(1)}, u32[]{:S(2)}, u32[]{:S(2)}) collective-permute-start(bf16[64,1792]{1,0:T(8,128)(2,1)S(1)} %slice.19), channel_id=1, source_target_pairs={{0,192},{64,0},{128,64},{192,128},{1,193},{65,1},{129,65},{193,129... | collective-permute-start | bytes 688136 | tf_op jit(solution)/shard_map/ppermute | solution.py:27
  185.8 7.9 %collective-permute-start.38 = (bf16[64,1792]{1,0:T(8,128)(2,1)S(1)}, bf16[64,1792]{1,0:T(8,128)(2,1)}, u32[]{:S(2)}, u32[]{:S(2)}) collective-permute-start(bf16[64,1792]{1,0:T(8,128)(2,1)S(1)} %slice.18), channel_id=1, source_target_pairs={{0,64},{64,128},{128,192},{192,0},{1,65},{65,129},{129,193},{193,1... | collective-permute-start | bytes 688136 | tf_op jit(solution)/shard_map/ppermute | solution.py:27
  193.6 2.9 %collective-permute-start.40 = (bf16[64,1792]{1,0:T(8,128)(2,1)}, bf16[64,1792]{1,0:T(8,128)(2,1)S(1)}, u32[]{:S(2)}, u32[]{:S(2)}) collective-permute-start(bf16[64,1792]{1,0:T(8,128)(2,1)} %collective-permute-done.38.refs_0_), channel_id=1, source_target_pairs={{0,32},{32,0},{1,33},{33,1},{2,34},{34,2},{3,35},{35,3},{4,36},{36... | collective-permute-start | bytes 688136 | tf_op jit(solution)/shard_map/ppermute | solution.py:27
  195.2 1.7 collective-permute-start.41
  (12 other events, 33.0 us)
